TPU v7x, 256 devices: a whole 4x4x8 slice. The times are simulated.
256 devices in a mesh: tensor: 4 (over y), expert: 32 (over z, x), dp: 2 (over core).
Axes of the slice: x: 4, y: 4, z: 8, core: 2. Of those that a mesh axis runs over, the one named last changes fastest.
Arguments:
- tokens: bfloat16 [8192, 2048], P(('dp', 'expert'), 'tensor'), parts along dimension 0, may hold values from -6 to 6
- expert_ids: int32 [8192, 8], P(('dp', 'expert')), parts along dimension 0, may hold values from 0 to 127, as said below
- combine_weight: bfloat16 [8192, 8], P(('dp', 'expert')), parts along dimension 0, may hold values from 0.049804688 to 1
- gate_weight: bfloat16 [128, 768, 2048], P('expert', 'tensor'), may hold values from -0.125 to 0.125
- up_weight: bfloat16 [128, 768, 2048], P('expert', 'tensor'), may hold values from -0.125 to 0.125
- down_weight: bfloat16 [128, 768, 2048], P('expert', 'tensor'), may hold values from -0.21875 to 0.21875
Outputs:
- mixed: bfloat16 [8192, 2048], P(('dp', 'expert'), 'tensor'), parts along dimension 0
There are 2 independent parts, one for each index of `dp`. A program takes and returns all parts, laid end to end along the dimension named above; an argument that names none is the same for every part. Nothing has to cross between parts.
Inputs may be any that keep to these rules, and one draw needn't show every extreme that they name: `expert_ids`: each row names 8 different experts; expert e sits on index e // 4 of expert. The experts of one row sit on exactly 6 different indices, at most 2 on one index. Among the rows of one index of expert (aligned blocks of 128 rows), at most 48 rows name experts on any one index, and in every draw some index receives exactly 48 rows from every block. Over all blocks at most 768 rows name any one expert, and in every draw some expert is named by exactly 768 rows.
All inputs are finite; a program needn't handle non-finite values.
Results may differ from a plain program's by a relative error of at most 0.0098.
Values may be sent and summed in bfloat16 or wider, within the bound.
A program may use at most 128 MiB of HBM per device.

v0:
```python
import jax
import jax.numpy as jnp
from jax import lax
from jax.sharding import PartitionSpec as P


def project_rows(inputs, weight_rows):
    return lax.dot_general(
        inputs, weight_rows, (((1,), (1,)), ((), ())), preferred_element_type=jnp.float32
    )


def per_device(tokens, expert_ids, combine_weight, gate_weight, up_weight, down_weight):
    dest_count = lax.axis_size("expert")
    tok_count = tokens.shape[0]
    local_count = gate_weight.shape[0]
    top_count = expert_ids.shape[1]
    spread = min(6, dest_count // 2)
    capacity = min(tok_count * 3 // 4, 2 * tok_count * spread // dest_count)
    most_share = (top_count + spread - 1) // spread
    expert_cap = dest_count * (capacity * most_share // local_count)
    owner_device = expert_ids // local_count
    dest_index = lax.broadcasted_iota(jnp.int32, (1, 1, dest_count), 2)
    present = jnp.max((owner_device[:, :, None] == dest_index).astype(jnp.int32), axis=1)
    before = jnp.cumsum(present, axis=0) - present
    slot_index = jnp.where(present > 0, before, capacity)
    cap_index = lax.broadcasted_iota(jnp.int32, (dest_count, capacity, tok_count), 1)
    placed = slot_index.T[:, None, :] == cap_index
    select = placed.reshape(dest_count * capacity, tok_count)
    expert_index = lax.broadcasted_iota(jnp.int32, (1, 1, dest_count * local_count), 2)
    dense_weight = jnp.sum(
        jnp.where(
            expert_ids[:, :, None] == expert_index,
            combine_weight[:, :, None].astype(jnp.float32),
            0.0,
        ),
        axis=1,
    )
    slot_weight = jnp.einsum(
        "jct,tjk->jck",
        placed.astype(jnp.float32),
        dense_weight.reshape(tok_count, dest_count, local_count),
        precision=lax.Precision.HIGHEST,
    ).astype(jnp.bfloat16)
    outgoing = jnp.dot(
        select.astype(jnp.bfloat16), tokens, preferred_element_type=jnp.float32
    ).astype(jnp.bfloat16)
    outgoing = outgoing.reshape(dest_count, capacity, outgoing.shape[-1])
    incoming = lax.all_to_all(outgoing, "expert", split_axis=0, concat_axis=0, tiled=True)
    weights_in = lax.all_to_all(slot_weight, "expert", split_axis=0, concat_axis=0, tiled=True)
    incoming = lax.all_gather(incoming, "tensor", axis=2, tiled=True)
    slot_count = incoming.shape[1]
    flat_rows = incoming.reshape(dest_count * slot_count, incoming.shape[2])
    row_total = flat_rows.shape[0]
    weight_flat = weights_in.reshape(row_total, local_count).astype(jnp.float32)
    row_ids = jnp.arange(row_total, dtype=jnp.int32)
    combined = jnp.zeros((row_total, flat_rows.shape[1]), jnp.float32)
    for expert_slot in range(local_count):
        column = weight_flat[:, expert_slot]
        live = column != 0.0
        live_count = live.astype(jnp.int32)
        position = jnp.cumsum(live_count) - live_count
        target = jnp.where(live, position, expert_cap)
        source = jnp.full((expert_cap,), row_total, jnp.int32).at[target].set(row_ids, mode="drop")
        valid = source < row_total
        safe_source = jnp.minimum(source, row_total - 1)
        rows_in = flat_rows[safe_source]
        row_weight = jnp.where(valid, column[safe_source], 0.0)
        gate_value = project_rows(rows_in, gate_weight[expert_slot])
        up_value = project_rows(rows_in, up_weight[expert_slot])
        hidden = (jax.nn.silu(gate_value) * up_value).astype(jnp.bfloat16)
        expert_out = jnp.dot(hidden, down_weight[expert_slot], preferred_element_type=jnp.float32)
        combined = combined.at[source].add(row_weight[:, None] * expert_out, mode="drop")
    combined = combined.reshape(dest_count, slot_count, flat_rows.shape[1])
    summed = lax.psum_scatter(
        combined.astype(jnp.bfloat16), "tensor", scatter_dimension=2, tiled=True
    ).astype(jnp.float32)
    returned_rows = lax.all_to_all(
        summed.astype(jnp.bfloat16), "expert", split_axis=0, concat_axis=0, tiled=True
    ).astype(summed.dtype)
    flat_back = returned_rows.reshape(dest_count * capacity, returned_rows.shape[2])
    dest_column = lax.broadcasted_iota(jnp.int32, (tok_count, dest_count), 1)
    flat_slot = jnp.where(present > 0, dest_column * capacity + before, dest_count * capacity)
    token_column = lax.broadcasted_iota(jnp.int32, (tok_count, dest_count), 0)
    slot_owner = (
        jnp.full((dest_count * capacity,), tok_count, jnp.int32)
        .at[flat_slot.reshape(-1)]
        .set(token_column.reshape(-1), mode="drop")
    )
    gathered = (
        jnp.zeros((tok_count, flat_back.shape[1]), jnp.float32)
        .at[slot_owner]
        .add(flat_back, mode="drop")
    )
    return gathered.astype(jnp.bfloat16)


def solution(mesh):
    in_specs = (
        P(("dp", "expert"), "tensor"),
        P(("dp", "expert"), None),
        P(("dp", "expert"), None),
        P("expert", "tensor", None),
        P("expert", "tensor", None),
        P("expert", "tensor", None),
    )
    out_specs = P(("dp", "expert"), "tensor")
    return jax.shard_map(
        per_device, mesh=mesh, in_specs=in_specs, out_specs=out_specs, check_vma=False
    )
```

profile of v0, /device:TPU:4, one launch (start us, length us, event | category | flops | bytes accessed | tf_op | source)
XLA Modules:
  0.0 449.6 jit_solution(14786095482715324377)
XLA Ops:
  6.5 0.7 add_select_fusion.1
  7.4 0.2 reduce_window_sum.84
  7.7 0.3 bitcast_compare_fusion
  8.1 0.6 convolution_convert_fusion
  8.6 50.8 %all_to_all.15 = bf16[32,48,512]{2,1,0:T(8,128)(2,1)} all-to-all(bf16[32,48,512]{2,1,0:T(8,128)(2,1)S(1)} %bitcast.106), channel_id=1, replica_groups=mesh['tensor'=4,'expert'=32,'dp'=2] {'expert'}, dimensions={0} | all-to-all | bytes 3145728 | tf_op jit(solution)/shard_map/all_to_all | solution.py:49
  59.7 0.3 select_reduce_fusion
  60.2 0.7 convolution_convert_fusion.1
  60.9 13.1 %all_to_all.16 = bf16[32,48,4]{1,2,0:T(4,128)(2,1)S(1)} all-to-all(bf16[32,48,4]{1,2,0:T(4,128)(2,1)S(1)} %convolution_convert_fusion.1), channel_id=1, replica_groups=mesh['tensor'=4,'expert'=32,'dp'=2] {'expert'}, dimensions={0} | all-to-all | bytes 24576 | tf_op jit(solution)/shard_map/all_to_all | solution.py:50
  74.2 0.3 reduce-window.50
  74.6 0.3 reduce-window.48
  75.0 0.3 reduce-window.36
  75.4 0.3 reduce-window.34
  75.9 0.1 slice_reduce_fusion.1
  76.0 0.1 slice_reduce_fusion.2
  76.1 0.1 slice_reduce_fusion.3
  76.4 0.1 fusion.88
  76.5 6.2 %scatter_custom_fusion.1 = s32[768]{0:T(1024)S(1)} fusion(s32[1536]{0:T(1024)S(1)} %get-tuple-element.10, s32[1536]{0:T(1024)S(1)} %iota.47, s32[]{:T(128)} %constant.52.clone.1), kind=kCustom, calls=%fused_computation.176 | custom fusion | bytes 3076 | tf_op jit(solution)/shard_map/scatter | solution.py:64
  82.8 4.5 gather_fusion
  87.3 6.2 %scatter_custom_fusion.3 = s32[768]{0:T(1024)S(1)} fusion(s32[1536]{0:T(1024)S(1)} %get-tuple-element.11, s32[1536]{0:T(1024)S(1)} %iota.51, s32[]{:T(128)} %constant.52.clone.1), kind=kCustom, calls=%fused_computation.174 | custom fusion | bytes 3076 | tf_op jit(solution)/shard_map/scatter | solution.py:64
  93.5 4.5 gather_fusion.2
  98.0 6.2 %scatter_custom_fusion.5 = s32[768]{0:T(1024)S(1)} fusion(s32[1536]{0:T(1024)S(1)} %get-tuple-element.12, s32[1536]{0:T(1024)S(1)} %iota.52, s32[]{:T(128)} %constant.52.clone.1), kind=kCustom, calls=%fused_computation.172 | custom fusion | bytes 3076 | tf_op jit(solution)/shard_map/scatter | solution.py:64
  104.2 4.5 gather_fusion.4
  108.7 6.4 %scatter_custom_fusion.7 = s32[768]{0:T(1024)S(1)} fusion(s32[1536]{0:T(1024)S(1)} %get-tuple-element.9, s32[1536]{0:T(1024)S(1)} %iota.53, s32[]{:T(128)} %constant.52.clone.1), kind=kCustom, calls=%fused_computation.170 | custom fusion | bytes 3076 | tf_op jit(solution)/shard_map/scatter | solution.py:64
  115.1 4.5 gather_fusion.6
  119.6 5.1 %all-gather.2.cloned.1.call-done = bf16[32,48,2048]{2,1,0:T(8,128)(2,1)} async-done(((bf16[32,48,512]{2,1,0:T(8,128)(2,1)}), bf16[32,48,2048]{2,1,0:T(8,128)(2,1)}) %all-gather.2.cloned.1.call-update) | async-done | bytes 6291472 | tf_op jit(solution)/shard_map/all_gather | solution.py:51
  124.7 10.7 %gather_fusion.1 = bf16[768,2048]{1,0:T(8,128)(2,1)} fusion(bf16[1536,2048]{1,0:T(8,128)(2,1)} %bitcast.100, s32[1024]{0:T(1024)S(1)} %pad_clamp_fusion.3), kind=kCustom, calls=%fused_computation.1 | custom fusion | bytes 6294528 | tf_op jit(solution)/shard_map/gather | solution.py:67
  135.4 10.7 %gather_fusion.3 = bf16[768,2048]{1,0:T(8,128)(2,1)} fusion(bf16[1536,2048]{1,0:T(8,128)(2,1)} %bitcast.101, s32[1024]{0:T(1024)S(1)} %pad_clamp_fusion.2), kind=kCustom, calls=%fused_computation.3 | custom fusion | bytes 6294528 | tf_op jit(solution)/shard_map/gather | solution.py:67
  146.1 10.8 %gather_fusion.5 = bf16[768,2048]{1,0:T(8,128)(2,1)} fusion(bf16[1536,2048]{1,0:T(8,128)(2,1)} %bitcast.102, s32[1024]{0:T(1024)S(1)} %pad_clamp_fusion.1), kind=kCustom, calls=%fused_computation.5 | custom fusion | bytes 6294528 | tf_op jit(solution)/shard_map/gather | solution.py:67
  156.9 10.3 %gather_fusion.7 = bf16[768,2048]{1,0:T(8,128)(2,1)S(1)} fusion(bf16[1536,2048]{1,0:T(8,128)(2,1)} %bitcast.103, s32[1024]{0:T(1024)S(1)} %pad_clamp_fusion), kind=kCustom, calls=%fused_computation.7 | custom fusion | bytes 6294528 | tf_op jit(solution)/shard_map/gather | solution.py:67
  167.2 4.2 fusion.41
  171.5 3.2 fusion.36
  174.6 7.5 %fusion.22 = f32[768,2048]{1,0:T(8,128)} fusion(bf16[768,2048]{1,0:T(8,128)(2,1)} %gather_fusion.1, bf16[4,192,2048]{2,1,0:T(8,128)(2,1)} %param.11, bf16[4,192,2048]{2,1,0:T(8,128)(2,1)} %param.10, f32[768,192]{0,1:T(8,128)} %fusion.41), kind=kOutput, calls=%fused_computation.45 | convolution fusion | flops 1208844288 | bytes 11599872 | tf_op jit(solution)/shard_map/dot_general | solution.py:72
  182.2 7.5 %fusion.21 = f32[768,2048]{1,0:T(8,128)} fusion(bf16[768,2048]{1,0:T(8,128)(2,1)} %gather_fusion.3, bf16[4,192,2048]{2,1,0:T(8,128)(2,1)} %param.11, bf16[4,192,2048]{2,1,0:T(8,128)(2,1)} %param.10, f32[768,192]{0,1:T(8,128)} %fusion.36), kind=kOutput, calls=%fused_computation.44 | convolution fusion | flops 1208844288 | bytes 11599872 | tf_op jit(solution)/shard_map/dot_general | solution.py:72
  189.7 4.1 fusion.31
  193.8 7.6 %fusion.20 = f32[768,2048]{1,0:T(8,128)} fusion(bf16[768,2048]{1,0:T(8,128)(2,1)} %gather_fusion.5, bf16[4,192,2048]{2,1,0:T(8,128)(2,1)} %param.11, bf16[4,192,2048]{2,1,0:T(8,128)(2,1)} %param.10, f32[768,192]{0,1:T(8,128)} %fusion.31), kind=kOutput, calls=%fused_computation.43 | convolution fusion | flops 1208844288 | bytes 11599872 | tf_op jit(solution)/shard_map/dot_general | solution.py:72
  201.4 3.1 fusion.26
  204.6 6.7 %fusion.19 = f32[768,2048]{1,0:T(8,128)} fusion(bf16[768,2048]{1,0:T(8,128)(2,1)S(1)} %gather_fusion.7, bf16[4,192,2048]{2,1,0:T(8,128)(2,1)} %param.11, bf16[4,192,2048]{2,1,0:T(8,128)(2,1)} %param.10, f32[768,192]{0,1:T(8,128)} %fusion.26), kind=kOutput, calls=%fused_computation.42 | convolution fusion | flops 1208844288 | bytes 11599872 | tf_op jit(solution)/shard_map/dot_general | solution.py:72
  211.3 21.0 %scatter_custom_fusion.2 = f32[1536,2048]{1,0:T(8,128)} fusion(s32[768]{0:T(1024)S(1)} %get-tuple-element.26, f32[768,2048]{1,0:T(8,128)} %fusion.22, f32[]{:T(128)} %constant.19.clone.1, f32[768]{0:T(1024)S(1)} %compare_select_fusion.21), kind=kCustom, calls=%fused_computation.24 | custom fusion | flops 3145728 | bytes 18878468 | tf_op jit(solution)/shard_map/scatter-add | solution.py:73
  232.3 24.8 %scatter_custom_fusion.4 = f32[1536,2048]{1,0:T(8,128)} fusion(f32[1536,2048]{1,0:T(8,128)} %scatter_custom_fusion.2, s32[768]{0:T(1024)S(1)} %get-tuple-element.24, f32[768,2048]{1,0:T(8,128)} %fusion.21, f32[768]{0:T(1024)S(1)} %compare_select_fusion.20), kind=kCustom, calls=%fused_computation.22 | custom fusion | flops 3145728 | bytes 18878464 | tf_op jit(solution)/shard_map/scatter-add | solution.py:73
  257.1 24.8 %scatter_custom_fusion.6 = f32[1536,2048]{1,0:T(8,128)} fusion(f32[1536,2048]{1,0:T(8,128)} %scatter_custom_fusion.4, s32[768]{0:T(1024)S(1)} %get-tuple-element.22, f32[768,2048]{1,0:T(8,128)} %fusion.20, f32[768]{0:T(1024)S(1)} %compare_select_fusion.19), kind=kCustom, calls=%fused_computation.20 | custom fusion | flops 3145728 | bytes 18878464 | tf_op jit(solution)/shard_map/scatter-add | solution.py:73
  281.9 24.9 %scatter_custom_fusion.8 = f32[1536,2048]{1,0:T(8,128)} fusion(f32[1536,2048]{1,0:T(8,128)} %scatter_custom_fusion.6, s32[768]{0:T(1024)S(1)} %get-tuple-element.20, f32[768,2048]{1,0:T(8,128)} %fusion.19, f32[768]{0:T(1024)S(1)} %compare_select_fusion.18), kind=kCustom, calls=%fused_computation.18 | custom fusion | flops 3145728 | bytes 18878464 | tf_op jit(solution)/shard_map/scatter-add | solution.py:73
  306.8 8.2 %convert_element_type.107 = bf16[1536,2048]{1,0:T(8,128)(2,1)} convert(f32[1536,2048]{1,0:T(8,128)} %scatter_custom_fusion.8) | non-fusion elementwise | flops 3145728 | bytes 18874368 | tf_op jit(solution)/shard_map/convert_element_type | solution.py:76
  315.0 67.4 %reduce-scatter.2.cloned.1.call-done = bf16[32,48,512]{2,1,0:T(8,128)(2,1)} async-done(((bf16[32,48,2048]{2,1,0:T(8,128)(2,1)}), bf16[32,48,512]{2,1,0:T(8,128)(2,1)}) %reduce-scatter.2.cloned.1.call-update) | async-done | bytes 1572880 | tf_op jit(solution)/shard_map/reduce_scatter | solution.py:75
  382.4 10.1 %all-to-all-start.2 = ((bf16[32,48,512]{2,1,0:T(8,128)(2,1)}), bf16[32,48,512]{2,1,0:T(8,128)(2,1)S(1)}, u32[]{:S(2)}, u32[]{:S(2)}) async-start(bf16[32,48,512]{2,1,0:T(8,128)(2,1)} %reduce-scatter.2.cloned.1.call-done), calls=%async_computation.3 | async-start | bytes 3145728 | tf_op jit(solution)/shard_map/all_to_all | solution.py:78
  392.7 15.5 %scatter_custom_fusion = s32[1536]{0:T(1024)S(1)} fusion(s32[4096]{0:T(1024)S(1)} %bitcast.112, s32[4096]{0:T(1024)S(1)} %reshape.318, s32[]{:T(128)} %constant.20.clone.1), kind=kCustom, calls=%fused_computation.159 | custom fusion | bytes 6148 | tf_op jit(solution)/shard_map/scatter | solution.py:88
  408.3 23.5 %all-to-all-done.2 = bf16[32,48,512]{2,1,0:T(8,128)(2,1)S(1)} async-done(((bf16[32,48,512]{2,1,0:T(8,128)(2,1)}), bf16[32,48,512]{2,1,0:T(8,128)(2,1)S(1)}, u32[]{:S(2)}, u32[]{:S(2)}) %all-to-all-start.2) | async-done | bytes 1572896 | tf_op jit(solution)/shard_map/all_to_all | solution.py:78
  431.8 9.8 %scatter_custom_fusion.9 = f32[128,512]{1,0:T(8,128)S(1)} fusion(s32[1536]{0:T(1024)S(1)} %compare_select_fusion.5, bf16[1536,512]{1,0:T(8,128)(2,1)S(1)} %bitcast.105, f32[]{:T(128)} %constant.19.clone.1), kind=kCustom, calls=%fused_computation.27 | custom fusion | flops 1572864 | bytes 1835012 | tf_op jit(solution)/shard_map/scatter-add | solution.py:93
  441.6 0.7 convert_element_type.109
  (60 shorter events, 1.9 us)
Async XLA Ops:
  6.5 1.5 copy-start
  6.5 118.2 %all-gather.2.cloned.1.call-start = ((), (), s32[]{:S(2)}) async-start(), calls=%async_computation.4 | async-start | bytes 7864320 | tf_op jit(solution)/shard_map/all_gather | solution.py:51
  8.0 51.5 %copy-start.3 = (s32[128,8]{0,1:T(8,128)S(1)}, s32[128,8]{0,1:T(8,128)}, u32[]{:S(2)}) copy-start(s32[128,8]{0,1:T(8,128)} %param.7) | copy-start | bytes 12292
  8.1 51.6 %copy-start.4 = (bf16[128,8]{0,1:T(8,128)(2,1)S(1)}, bf16[128,8]{0,1:T(8,128)(2,1)}, u32[]{:S(2)}) copy-start(bf16[128,8]{0,1:T(8,128)(2,1)} %param.8) | copy-start | bytes 6148
  59.4 322.9 %reduce-scatter.2.cloned.1.call-start = ((), (), s32[]{:S(2)}) async-start(), calls=%async_computation.5 | async-start | bytes 7864320 | tf_op jit(solution)/shard_map/reduce_scatter | solution.py:75
  167.2 4.2 copy-start.2
  315.0 127.3 %copy-start.1 = (bf16[128,512]{1,0:T(8,128)(2,1)S(1)}, bf16[128,512]{1,0:T(8,128)(2,1)}, u32[]{:S(2)}) copy-start(bf16[128,512]{1,0:T(8,128)(2,1)} %param.6) | copy-start | bytes 393220
  382.4 49.4 %all-to-all-start.2 = ((bf16[32,48,512]{2,1,0:T(8,128)(2,1)}), bf16[32,48,512]{2,1,0:T(8,128)(2,1)S(1)}, u32[]{:S(2)}, u32[]{:S(2)}) async-start(bf16[32,48,512]{2,1,0:T(8,128)(2,1)} %reduce-scatter.2.cloned.1.call-done), calls=%async_computation.3 | async-start | bytes 3145728 | tf_op jit(solution)/shard_map/all_to_all | solution.py:78
Sparse Core Ops, SparseCore 0:
  59.6 65.1 all-gather.1
  315.1 67.1 reduce-scatter.1
where the time goes:
time: 457 us; the launch traced here: 450 us
  other arithmetic  117 us (26%)
  local copies, waits for them, and re-layouts  102 us (22%)
  waiting for transfers between devices  96 us (21%)
  blocking collectives  63.9 us (14%)
  matrix products  45.3 us (10%)
  between operations  14.3 us (3%)
  starting transfers between devices  10.2 us (2%)
    scatter-add x4, other arithmetic, per_device(): combined.at[source].add(row_weight[:, None] * expert_out, mode='drop')  95.5 us
    reduce_scatter x1, waiting for transfers between devices, per_device(): lax.psum_scatter(combined.astype(jnp.bfloat16), 'tensor', scatter_dimensi...  67.4 us
    all_to_all x1, blocking collectives, per_device(): lax.all_to_all(outgoing, 'expert', split_axis=0, concat_axis=0, tiled=True)  50.8 us
    gather x4, local copies, waits for them, and re-layouts, per_device(): rows_in = flat_rows[safe_source]  42.5 us
    dot_general x4, matrix products, per_device(): jnp.dot(hidden, down_weight[expert_slot], preferred_element_type=jnp.floa...  29.4 us
    scatter x4, local copies, waits for them, and re-layouts, per_device(): jnp.full((expert_cap,), row_total, jnp.int32).at[target]  24.9 us
    all_to_all x1, waiting for transfers between devices, per_device(): lax.all_to_all(summed.astype(jnp.bfloat16), 'expert', split_axis=0, conca...  23.5 us
    gather x4, local copies, waits for them, and re-layouts, per_device(): row_weight = jnp.where(valid, column[safe_source], 0.0)  17.9 us
  transfers between devices with their start and end apart: 3, of which 3 were waited for; matrix products, arithmetic and copies ran while one was open for 14% of the time, Pallas kernels for 0%

commit v1 on v0

v1 whole, which is shorter than its diff:
```python
import functools
import jax
import jax.numpy as jnp
from jax import lax
from jax.experimental import pallas as pl
from jax.experimental.pallas import tpu as pltpu
from jax.sharding import PartitionSpec as P

NT = 4
NX = 4
NZ = 8
TOK = 128
CAP = 48
ROWS = NX * CAP
SLICE = 512
CA = 384
CB = SLICE - CA
TW = CA + NT * CB
XW = TW + 128
HID = 768
DM = NT * SLICE
LAST = NZ - 1
BF = jnp.bfloat16
F32 = jnp.float32


def dot(a, b, dims=((1,), (0,))):
    return lax.dot_general(a, b, (dims, ((), ())), preferred_element_type=F32)


def kernel(
    tok_ref, meta_ref, gate_hbm, up_hbm, down_hbm, out_ref,
    wg, wu, wd, expand, t_buf, m_buf, sel, xs_buf, xr_buf, x_buf, x_all, hid,
    p_buf, r1_buf, r2_buf, q_buf, xb_buf, zs_buf, zb_buf, acc, bs_buf, br_buf,
    w_sem, z_send, z_recv, m_send, m_recv, x_send, x_recv,
    a1_send, a1_recv, a2_send, a2_recv, r1_send, r1_recv, r2_send, r2_recv,
    xb_send, xb_recv, zb_send, zb_recv, b_send, b_recv, bb_send, bb_recv,
):
    y = lax.axis_index("tensor")
    e = lax.axis_index("expert")
    z = e // NX
    x = e % NX
    yp = (y + 1) % NT
    yo = (y + 2) % NT
    ym = (y + 3) % NT

    def at_y(j):
        return {"tensor": j}

    def at_x(j):
        return {"expert": z * NX + j}

    def at_z(j):
        return {"expert": j * NX + x}

    def rcopy(src, dst, ssem, rsem, dev):
        return pltpu.make_async_remote_copy(
            src_ref=src, dst_ref=dst, send_sem=ssem, recv_sem=rsem,
            device_id=dev, device_id_type=pl.DeviceIdType.MESH,
        )

    def rows48(j):
        return pl.ds(pl.multiple_of(j * CAP, 16), CAP)

    def bcol(j):
        return pl.ds(pl.multiple_of(CA + CB * j, 128), CB)

    def z_copies(src, slot, dev):
        return (
            rcopy(t_buf.at[src], t_buf.at[slot], z_send.at[slot], z_recv.at[slot], dev),
            rcopy(m_buf.at[src], m_buf.at[slot], m_send.at[slot], m_recv.at[slot], dev),
        )

    def x_copy(c, r):
        to = (x + r) % NX
        return rcopy(
            xs_buf.at[c, rows48(to)], xr_buf.at[c, rows48(x)],
            x_send.at[c, r - 1], x_recv.at[c, r - 1], at_x(to),
        )

    def x_arrival(c, r):
        frm = (x + NX - r) % NX
        return rcopy(
            xs_buf.at[c, rows48(frm)], xr_buf.at[c, rows48(frm)],
            x_send.at[c, r - 1], x_recv.at[c, r - 1], at_x(frm),
        )

    def a1_copy(c, k):
        return rcopy(
            xr_buf.at[c, :, pl.ds(0, CA)], x_buf.at[c, y],
            a1_send.at[c, k], a1_recv.at[c, k], at_y(ym if k else yp),
        )

    def a1_arrival(c, k):
        frm = yp if k else ym
        return rcopy(
            xr_buf.at[c, :, pl.ds(0, CA)], x_buf.at[c, frm],
            a1_send.at[c, k], a1_recv.at[c, k], at_y(frm),
        )

    half = ROWS // 2

    def a2_copy(c, k):
        blk = x_buf.at[c, yp if k else ym, pl.ds(k * half, half)]
        return rcopy(blk, blk, a2_send.at[c, k], a2_recv.at[c, k], at_y(ym if k else yp))

    def a2_arrival(c, k):
        blk = x_buf.at[c, yo, pl.ds(k * half, half)]
        return rcopy(blk, blk, a2_send.at[c, k], a2_recv.at[c, k], at_y(yp if k else ym))

    def r1_copy(c, k):
        return rcopy(
            p_buf.at[c, yo, pl.ds(k * half, half), pl.ds(0, CA)], r1_buf.at[c, k],
            r1_send.at[c, k], r1_recv.at[c, k], at_y(ym if k else yp),
        )

    def r2_copy(c, k):
        to = ym if k else yp
        return rcopy(
            p_buf.at[c, to, :, pl.ds(0, CA)], r2_buf.at[c, k],
            r2_send.at[c, k], r2_recv.at[c, k], at_y(to),
        )

    def xb_copy(c, r):
        to = (x + r) % NX
        return rcopy(
            q_buf.at[c, rows48(to)], xb_buf.at[c, rows48(x)],
            xb_send.at[c, r - 1], xb_recv.at[c, r - 1], at_x(to),
        )

    def xb_arrival(c, r):
        frm = (x + NX - r) % NX
        return rcopy(
            q_buf.at[c, rows48(frm)], xb_buf.at[c, rows48(frm)],
            xb_send.at[c, r - 1], xb_recv.at[c, r - 1], at_x(frm),
        )

    def zb_copy(c):
        dist = (c + 1) // 2
        to = jnp.where(c % 2 == 1, z + NZ - dist, z + dist) % NZ
        return rcopy(zs_buf.at[c], zb_buf.at[c], zb_send.at[c], zb_recv.at[c], at_z(to))

    def b_copy(r):
        return rcopy(
            tok_ref.at[:, pl.ds(CA, CB)], t_buf.at[0, :, bcol(y)],
            b_send.at[r - 1], b_recv.at[r - 1], at_y((y + r) % NT),
        )

    def b_arrival(r):
        frm = (y + NT - r) % NT
        return rcopy(
            tok_ref.at[:, pl.ds(CA, CB)], t_buf.at[0, :, bcol(frm)],
            b_send.at[r - 1], b_recv.at[r - 1], at_y(frm),
        )

    def bb_copy(r):
        return rcopy(
            bs_buf.at[r - 1], br_buf.at[r - 1],
            bb_send.at[r - 1], bb_recv.at[r - 1], at_y((y + r) % NT),
        )

    loads = [
        pltpu.make_async_copy(src, dst, w_sem.at[k])
        for k, (src, dst) in enumerate(((gate_hbm, wg), (up_hbm, wu), (down_hbm, wd)))
    ]
    for load in loads:
        load.start()

    barrier = pltpu.get_barrier_semaphore()
    peers = [at_y((y + r) % NT) for r in range(1, NT)]
    peers += [at_x((x + r) % NX) for r in range(1, NX)]
    peers += [at_z((z + r) % NZ) for r in range(1, NZ)]
    for peer in peers:
        pl.semaphore_signal(barrier, 1, device_id=peer, device_id_type=pl.DeviceIdType.MESH)

    t_buf[0, :, 0:CA] = tok_ref[:, 0:CA]
    t_buf[0, :, bcol(y)] = tok_ref[:, CA:SLICE]
    m_buf[0] = meta_ref[...]
    lane_q = lax.broadcasted_iota(jnp.int32, (128, HID), 0)
    hid_n = lax.broadcasted_iota(jnp.int32, (128, HID), 1)
    base = (lane_q - NX * x) * (HID // NX)
    expand[...] = jnp.where((hid_n >= base) & (hid_n < base + HID // NX), 1.0, 0.0).astype(BF)

    pl.semaphore_wait(barrier, len(peers))
    for r in (1, 3, 2):
        b_copy(r).start()
    for r in (1, 3, 2):
        b_arrival(r).wait_recv()
    for cp in z_copies(0, 1, at_z((z + 1) % NZ)):
        cp.start()

    def route(c):
        meta = m_buf[c].astype(F32)
        rel = meta[0:8] - jnp.asarray(NX * NX * z, F32)
        wts = meta[8:16]
        sub16 = lax.broadcasted_iota(jnp.int32, (16, TOK), 0)
        present = jnp.zeros((16, TOK), F32)
        rows = []
        for xx in range(NX):
            inside = (rel >= float(NX * xx)) & (rel < float(NX * xx + NX))
            row = jnp.max(jnp.where(inside, 1.0, 0.0), axis=0, keepdims=True)
            rows.append(row)
            present = jnp.where(sub16 == xx, row, present)
        t0 = lax.broadcasted_iota(jnp.int32, (TOK, TOK), 0)
        t1 = lax.broadcasted_iota(jnp.int32, (TOK, TOK), 1)
        earlier = jnp.where(t0 < t1, 1.0, 0.0).astype(BF)
        before = dot(present.astype(BF), earlier)
        slot = lax.broadcasted_iota(jnp.int32, (CAP, TOK), 0).astype(F32)
        for xx in range(NX):
            hit = (slot == before[xx : xx + 1]) & (rows[xx] > 0.5)
            sel[c, xx * CAP : (xx + 1) * CAP] = jnp.where(hit, 1.0, 0.0).astype(BF)
        sub = t0.astype(F32)
        wide = jnp.zeros((TOK, TOK), F32)
        for i in range(8):
            wide = jnp.where(sub == rel[i : i + 1], wts[i : i + 1], wide)
        s = sel[c]
        xs_buf[c, :, 0:TW] = dot(s, t_buf[c]).astype(BF)
        xs_buf[c, :, TW:XW] = dot(s, wide.astype(BF), ((1,), (1,))).astype(BF)
        xr_buf[c, rows48(x)] = xs_buf[c, rows48(x)]

    def experts(c):
        for j in range(NT):
            x_all[:, j * SLICE : j * SLICE + CA] = x_buf[c, j]
            x_all[:, j * SLICE + CA : (j + 1) * SLICE] = xr_buf[c, :, CA + CB * j : CA + CB * (j + 1)]
        rows_in = x_all[...]
        slot_w = xr_buf[c, :, TW:XW]
        for n in range(HID // 256):
            cols = slice(n * 256, (n + 1) * 256)
            gate = dot(rows_in, wg[cols], ((1,), (1,)))
            up = dot(rows_in, wu[cols], ((1,), (1,)))
            scale = dot(slot_w, expand[:, cols])
            hid[:, cols] = (gate / (1.0 + jnp.exp(-gate)) * up * scale).astype(BF)
        h = hid[...]
        for j in range(NT):
            for n in range(SLICE // 256):
                lo = j * SLICE + n * 256
                p_buf[c, j, :, n * 256 : (n + 1) * 256] = dot(h, wd[:, lo : lo + 256]).astype(BF)

    def on(c):
        return (c >= 0) & (c < NZ)

    def step(i, carry):
        c3 = i - 2

        @pl.when(on(c3))
        def _():
            for k in range(2):
                a1_arrival(c3, k).wait_recv()
                a2_copy(c3, k).start()

        c2 = i - 1

        @pl.when(on(c2))
        def _():
            for r in (1, 3, 2):
                x_arrival(c2, r).wait_recv()
            for k in range(2):
                a1_copy(c2, k).start()
            x_buf[c2, y] = xr_buf[c2, :, 0:CA]

        c5 = i - 4

        @pl.when(on(c5))
        def _():
            for k in range(2):
                to = ym if k else yp
                part = slice(k * half, (k + 1) * half)
                r1_copy(c5, k).wait_recv()
                p_buf[c5, to, part, 0:CA] = (
                    p_buf[c5, to, part, 0:CA].astype(F32) + r1_buf[c5, k].astype(F32)
                ).astype(BF)
                r2_copy(c5, k).start()

        c1 = i

        @pl.when(on(c1))
        def _():
            @pl.when(c1 > 0)
            def _():
                for cp in z_copies(0, c1, at_z(z)):
                    cp.wait_recv()

            @pl.when(c1 < NZ - 2)
            def _():
                dz = jnp.where(c1 % 2 == 1, 1, NZ - 1)
                for cp in z_copies(c1, c1 + 2, at_z((z + dz) % NZ)):
                    cp.start()

            route(c1)
            for r in (1, 3, 2):
                x_copy(c1, r).start()

        c6 = i - 5

        @pl.when(on(c6))
        def _():
            for k in range(2):
                r2_copy(c6, k).wait_recv()
            q_buf[c6, :, 0:CA] = (
                p_buf[c6, y, :, 0:CA].astype(F32)
                + r2_buf[c6, 0].astype(F32)
                + r2_buf[c6, 1].astype(F32)
            ).astype(BF)
            for j in range(NT):
                q_buf[c6, :, CA + CB * j : CA + CB * (j + 1)] = p_buf[c6, j, :, CA:SLICE]
            for r in (1, 3, 2):
                xb_copy(c6, r).start()
            xb_buf[c6, rows48(x)] = q_buf[c6, rows48(x)]

        c7 = i - 6

        @pl.when(on(c7))
        def _():
            for r in (1, 3, 2):
                xb_arrival(c7, r).wait_recv()
            share = dot(sel[c7], xb_buf[c7], ((0,), (0,)))

            @pl.when(c7 == 0)
            def _():
                acc[...] = share

            @pl.when(c7 > 0)
            def _():
                zs_buf[c7] = share.astype(BF)
                zb_copy(c7).start()

        c8 = i - 7

        @pl.when((c8 >= 1) & (c8 < NZ))
        def _():
            zb_copy(c8).wait_recv()
            acc[...] += zb_buf[c8].astype(F32)

        c4 = i - 3

        @pl.when(c4 == 0)
        def _():
            for load in loads:
                load.wait()

        @pl.when(on(c4))
        def _():
            for k in range(2):
                a2_arrival(c4, k).wait_recv()
            experts(c4)
            for k in range(2):
                r1_copy(c4, k).start()

        return carry

    lax.fori_loop(0, NZ + 7, step, 0)

    for r in (1, 3, 2):
        bs_buf[r - 1] = acc[:, bcol((y + r) % NT)].astype(BF)
        bb_copy(r).start()
    out_ref[:, 0:CA] = acc[:, 0:CA].astype(BF)
    total = acc[:, bcol(y)]
    for r in (1, 3, 2):
        bb_copy(r).wait_recv()
        total = total + br_buf[r - 1].astype(F32)
    out_ref[:, CA:SLICE] = total.astype(BF)

    def drain(c, carry):
        for k in range(2):
            a1_copy(c, k).wait_send()
            a2_copy(c, k).wait_send()
            r1_copy(c, k).wait_send()
            r2_copy(c, k).wait_send()
        for r in range(1, NX):
            x_copy(c, r).wait_send()
            xb_copy(c, r).wait_send()

        @pl.when(c > 0)
        def _():
            for cp in z_copies(0, c, at_z(z)):
                cp.wait_send()
            zb_copy(c).wait_send()

        return carry

    lax.fori_loop(0, NZ, drain, 0)
    for r in range(1, NT):
        b_copy(r).wait_send()
        bb_copy(r).wait_send()


def per_device(tokens, expert_ids, combine_weight, gate_weight, up_weight, down_weight):
    meta = jnp.concatenate([expert_ids.astype(BF), combine_weight], axis=1).T
    flat = (HID, DM)
    vmem = pl.BlockSpec(memory_space=pltpu.VMEM)
    hbm = pl.BlockSpec(memory_space=pl.ANY)
    dma = pltpu.SemaphoreType.DMA
    return pl.pallas_call(
        kernel,
        out_shape=jax.ShapeDtypeStruct((TOK, SLICE), BF),
        in_specs=[vmem, vmem, hbm, hbm, hbm],
        out_specs=vmem,
        scratch_shapes=[
            pltpu.VMEM(flat, BF), pltpu.VMEM(flat, BF), pltpu.VMEM(flat, BF),
            pltpu.VMEM((128, HID), BF),
            pltpu.VMEM((NZ, TOK, TW), BF),
            pltpu.VMEM((NZ, 16, TOK), BF),
            pltpu.VMEM((NZ, ROWS, TOK), BF),
            pltpu.VMEM((NZ, ROWS, XW), BF),
            pltpu.VMEM((NZ, ROWS, XW), BF),
            pltpu.VMEM((NZ, NT, ROWS, CA), BF),
            pltpu.VMEM((ROWS, DM), BF),
            pltpu.VMEM((ROWS, HID), BF),
            pltpu.VMEM((NZ, NT, ROWS, SLICE), BF),
            pltpu.VMEM((NZ, 2, ROWS // 2, CA), BF),
            pltpu.VMEM((NZ, 2, ROWS, CA), BF),
            pltpu.VMEM((NZ, ROWS, TW), BF),
            pltpu.VMEM((NZ, ROWS, TW), BF),
            pltpu.VMEM((NZ, TOK, TW), BF),
            pltpu.VMEM((NZ, TOK, TW), BF),
            pltpu.VMEM((TOK, TW), F32),
            pltpu.VMEM((NT - 1, TOK, CB), BF),
            pltpu.VMEM((NT - 1, TOK, CB), BF),
            dma((3,)),
            dma((NZ,)), dma((NZ,)), dma((NZ,)), dma((NZ,)),
            dma((NZ, 3)), dma((NZ, 3)),
            dma((NZ, 2)), dma((NZ, 2)), dma((NZ, 2)), dma((NZ, 2)),
            dma((NZ, 2)), dma((NZ, 2)), dma((NZ, 2)), dma((NZ, 2)),
            dma((NZ, 3)), dma((NZ, 3)),
            dma((NZ,)), dma((NZ,)),
            dma((3,)), dma((3,)), dma((3,)), dma((3,)),
        ],
        compiler_params=pltpu.CompilerParams(
            collective_id=0, has_side_effects=True, vmem_limit_bytes=60 * 2**20
        ),
        name="moe",
    )(
        tokens, meta, gate_weight.reshape(flat), up_weight.reshape(flat), down_weight.reshape(flat)
    )


def solution(mesh):
    in_specs = (
        P(("dp", "expert"), "tensor"),
        P(("dp", "expert"), None),
        P(("dp", "expert"), None),
        P("expert", "tensor", None),
        P("expert", "tensor", None),
        P("expert", "tensor", None),
    )
    out_specs = P(("dp", "expert"), "tensor")
    return jax.shard_map(
        per_device, mesh=mesh, in_specs=in_specs, out_specs=out_specs, check_vma=False
    )
```

time: 457 us -> 141 us (0.31); the launches traced: 450 us -> 141 us
  Pallas kernels: 0 us -> 137 us
  other arithmetic: 117 us -> 1.96 us
  local copies, waits for them, and re-layouts: 102 us -> 1.57 us
  waiting for transfers between devices: 96 us -> 0 us
  blocking collectives: 63.9 us -> 0 us
  matrix products: 45.3 us -> 0 us
  between operations: 14.3 us -> 0.01 us
  starting transfers between devices: 10.2 us -> 0 us
    pallas_call x0 -> x1, Pallas kernels: none -> 137 us  [per_device(): pl.pallas_call(kernel, out_shape=jax.ShapeDtypeStruct((TOK, SLICE), BF),...]
    scatter-add x5 -> x0, other arithmetic: 105 us -> none  [the longest x4 95.5 us: per_device(): combined.at[source].add(row_weight[:, None] * expert_out, mode='drop')]
    reduce_scatter x1 -> x0, waiting for transfers between devices: 67.4 us -> none  [per_device(): lax.psum_scatter(combined.astype(jnp.bfloat16), 'tensor', scatter_dimensi...]
    all_to_all x2 -> x0, blocking collectives: 63.9 us -> none  [the longest x1 50.8 us: per_device(): lax.all_to_all(outgoing, 'expert', split_axis=0, concat_axis=0, tiled=True)]
    gather x8 -> x0, local copies, waits for them, and re-layouts: 60.3 us -> none  [the longest x4 42.5 us: per_device(): rows_in = flat_rows[safe_source]]
    dot_general x10 -> x0, matrix products: 45.3 us -> none  [the longest x4 29.4 us: per_device(): jnp.dot(hidden, down_weight[expert_slot], preferred_element_type=jnp.floa...]
    scatter x5 -> x0, local copies, waits for them, and re-layouts: 40.4 us -> none  [the longest x4 24.9 us: per_device(): jnp.full((expert_cap,), row_total, jnp.int32).at[target]]
    all_to_all x1 -> x0, waiting for transfers between devices: 23.5 us -> none  [per_device(): lax.all_to_all(summed.astype(jnp.bfloat16), 'expert', split_axis=0, conca...]
  transfers between devices with their start and end apart: 3 -> 0, of which waited for: 3 -> 0; matrix products, arithmetic and copies ran while one was open for 14% -> 0% of each run, Pallas kernels for 0% -> 0%
where the time goes in v1:
time: 141 us
  Pallas kernels  137 us (97%)
  other arithmetic  1.96 us (1%)
  local copies, waits for them, and re-layouts  1.57 us (1%)
    pallas_call x1, Pallas kernels, per_device(): pl.pallas_call(kernel, out_shape=jax.ShapeDtypeStruct((TOK, SLICE), BF),...  137 us

profile of v1, /device:TPU:4, one launch (start us, length us, event | category | flops | bytes accessed | tf_op | source)
XLA Modules:
  0.0 140.7 jit_solution(5397420043121969006)
XLA Ops:
  0.0 0.7 convert_element_type.3
  0.7 1.3 maximum_bitcast_fusion.meta_ref
  2.0 137.2 %moe.1 = bf16[128,512]{1,0:T(8,128)(2,1)} custom-call(bf16[128,512]{1,0:T(8,128)(2,1)} %tok_ref.1, bf16[16,128]{1,0:T(8,128)(2,1)} %maximum_bitcast_fusion.meta_ref, bf16[768,2048]{1,0:T(8,128)(2,1)} %bitcast.5, bf16[768,2048]{1,0:T(8,128)(2,1)} %bitcast.6, bf16[768,2048]{1,0:T(8,128)(2,1)} %bitcast.7), custom_call_target="tpu_custom_call" | custom-call | tf_op jit(solution)/shard_map/moe/pallas_call | solution.py:393
  139.1 1.6 %copy.8 = bf16[128,512]{1,0:T(8,128)(2,1)} copy(bf16[128,512]{1,0:T(8,128)(2,1)} %moe.1) | data formatting | bytes 262144

commit v2 on v1

--- a/solution.py
+++ b/solution.py
@@ -1,4 +1,3 @@
-import functools
 import jax
 import jax.numpy as jnp
 from jax import lax
@@ -19,20 +18,32 @@
 XW = TW + 128
 HID = 768
 DM = NT * SLICE
-LAST = NZ - 1
 BF = jnp.bfloat16
 F32 = jnp.float32
 
+SLOTS = 33
+SCHEDULE = (
+    ("select", (0, 3, 2, 6, 12, 7, 9, 10)),
+    ("gather2", (6, 8, 7, 11, 16, 15, 14, 13)),
+    ("gather1", (2, 6, 5, 7, 14, 10, 11, 12)),
+    ("ffn", (28, 23, 14, 12, 18, 17, 16, 15)),
+    ("scatter2", (31, 29, 28, 27, 24, 22, 19, 18)),
+    ("merge", (-1, 32, 31, 30, 29, 26, 25, 21)),
+    ("forward", (-1, 1, 0, 4, 3, 6, -1, -1)),
+    ("scatter1", (30, 27, 23, 20, 19, 18, 17, 16)),
+    ("unselect", (32, 31, 30, 29, 28, 25, 24, 20)),
+)
+
 
 def dot(a, b, dims=((1,), (0,))):
     return lax.dot_general(a, b, (dims, ((), ())), preferred_element_type=F32)
 
 
 def kernel(
-    tok_ref, meta_ref, gate_hbm, up_hbm, down_hbm, out_ref,
+    tok_ref, ids_ref, comb_ref, gate_hbm, up_hbm, down_hbm, out_ref,
     wg, wu, wd, expand, t_buf, m_buf, sel, xs_buf, xr_buf, x_buf, x_all, hid,
-    p_buf, r1_buf, r2_buf, q_buf, xb_buf, zs_buf, zb_buf, acc, bs_buf, br_buf,
-    w_sem, z_send, z_recv, m_send, m_recv, x_send, x_recv,
+    p_buf, r1_buf, r2_buf, q_buf, xb_buf, share_buf, zs_buf, zb_buf, acc, bs_buf, br_buf,
+    w_sem, z_send, z_recv, zz_send, zz_recv, m_send, m_recv, x_send, x_recv,
     a1_send, a1_recv, a2_send, a2_recv, r1_send, r1_recv, r2_send, r2_recv,
     xb_send, xb_recv, zb_send, zb_recv, b_send, b_recv, bb_send, bb_recv,
 ):
@@ -66,9 +77,11 @@
         return pl.ds(pl.multiple_of(CA + CB * j, 128), CB)
 
     def z_copies(src, slot, dev):
+        one, two = pl.ds(0, CA), pl.ds(CA, TW - CA)
         return (
-            rcopy(t_buf.at[src], t_buf.at[slot], z_send.at[slot], z_recv.at[slot], dev),
             rcopy(m_buf.at[src], m_buf.at[slot], m_send.at[slot], m_recv.at[slot], dev),
+            rcopy(t_buf.at[src, :, one], t_buf.at[slot, :, one], z_send.at[slot], z_recv.at[slot], dev),
+            rcopy(t_buf.at[src, :, two], t_buf.at[slot, :, two], zz_send.at[slot], zz_recv.at[slot], dev),
         )
 
     def x_copy(c, r):
@@ -136,8 +149,7 @@
         )
 
     def zb_copy(c):
-        dist = (c + 1) // 2
-        to = jnp.where(c % 2 == 1, z + NZ - dist, z + dist) % NZ
+        to = jnp.where(c % 2 == 1, z + NZ - 1, z + 1) % NZ
         return rcopy(zs_buf.at[c], zb_buf.at[c], zb_send.at[c], zb_recv.at[c], at_z(to))
 
     def b_copy(r):
@@ -169,13 +181,18 @@
     barrier = pltpu.get_barrier_semaphore()
     peers = [at_y((y + r) % NT) for r in range(1, NT)]
     peers += [at_x((x + r) % NX) for r in range(1, NX)]
-    peers += [at_z((z + r) % NZ) for r in range(1, NZ)]
+    peers += [at_z((z + r) % NZ) for r in (1, NZ - 1)]
     for peer in peers:
         pl.semaphore_signal(barrier, 1, device_id=peer, device_id_type=pl.DeviceIdType.MESH)
 
     t_buf[0, :, 0:CA] = tok_ref[:, 0:CA]
     t_buf[0, :, bcol(y)] = tok_ref[:, CA:SLICE]
-    m_buf[0] = meta_ref[...]
+    d0 = lax.broadcasted_iota(jnp.int32, (TOK, TOK), 0)
+    d1 = lax.broadcasted_iota(jnp.int32, (TOK, TOK), 1)
+    unit = jnp.where(d0 == d1, 1.0, 0.0).astype(BF)
+    ids_t = dot(ids_ref[...].astype(F32).astype(BF), unit, ((0,), (0,)))
+    comb_t = dot(comb_ref[...], unit, ((0,), (0,)))
+    m_buf[0] = jnp.concatenate([ids_t, comb_t], axis=0).astype(BF)
     lane_q = lax.broadcasted_iota(jnp.int32, (128, HID), 0)
     hid_n = lax.broadcasted_iota(jnp.int32, (128, HID), 1)
     base = (lane_q - NX * x) * (HID // NX)
@@ -184,10 +201,13 @@
     pl.semaphore_wait(barrier, len(peers))
     for r in (1, 3, 2):
         b_copy(r).start()
-    for r in (1, 3, 2):
-        b_arrival(r).wait_recv()
-    for cp in z_copies(0, 1, at_z((z + 1) % NZ)):
-        cp.start()
+    own = (z_copies(0, 1, at_z((z + 1) % NZ)), z_copies(0, 2, at_z((z + NZ - 1) % NZ)))
+    for k in range(3):
+        if k == 2:
+            for r in (1, 3, 2):
+                b_arrival(r).wait_recv()
+        for cps in own:
+            cps[k].start()
 
     def route(c):
         meta = m_buf[c].astype(F32)
@@ -236,120 +256,112 @@
                 lo = j * SLICE + n * 256
                 p_buf[c, j, :, n * 256 : (n + 1) * 256] = dot(h, wd[:, lo : lo + 256]).astype(BF)
 
-    def on(c):
-        return (c >= 0) & (c < NZ)
+    def forward(c):
+        for cp in z_copies(0, c, at_z(z)):
+            cp.wait_recv()
+        dz = jnp.where(c % 2 == 1, 1, NZ - 1)
+        for cp in z_copies(c, c + 2, at_z((z + dz) % NZ)):
+            cp.start()
+
+    def select(c):
+        @pl.when(c >= NZ - 2)
+        def _():
+            for cp in z_copies(0, c, at_z(z)):
+                cp.wait_recv()
+
+        route(c)
+        for r in (1, 3, 2):
+            x_copy(c, r).start()
+
+    def gather1(c):
+        for r in (1, 3, 2):
+            x_arrival(c, r).wait_recv()
+        for k in range(2):
+            a1_copy(c, k).start()
+        x_buf[c, y] = xr_buf[c, :, 0:CA]
+
+    def gather2(c):
+        for k in range(2):
+            a1_arrival(c, k).wait_recv()
+            a2_copy(c, k).start()
+
+    def ffn(c):
+        for k in range(2):
+            a2_arrival(c, k).wait_recv()
+        experts(c)
+        for k in range(2):
+            r1_copy(c, k).start()
+
+    def scatter1(c):
+        for k in range(2):
+            to = ym if k else yp
+            part = slice(k * half, (k + 1) * half)
+            r1_copy(c, k).wait_recv()
+            p_buf[c, to, part, 0:CA] = (
+                p_buf[c, to, part, 0:CA].astype(F32) + r1_buf[c, k].astype(F32)
+            ).astype(BF)
+            r2_copy(c, k).start()
+
+    def scatter2(c):
+        for k in range(2):
+            r2_copy(c, k).wait_recv()
+        q_buf[c, :, 0:CA] = (
+            p_buf[c, y, :, 0:CA].astype(F32)
+            + r2_buf[c, 0].astype(F32)
+            + r2_buf[c, 1].astype(F32)
+        ).astype(BF)
+        for j in range(NT):
+            q_buf[c, :, CA + CB * j : CA + CB * (j + 1)] = p_buf[c, j, :, CA:SLICE]
+        for r in (1, 3, 2):
+            xb_copy(c, r).start()
+        xb_buf[c, rows48(x)] = q_buf[c, rows48(x)]
+
+    def unselect(c):
+        for r in (1, 3, 2):
+            xb_arrival(c, r).wait_recv()
+        share_buf[c] = dot(sel[c], xb_buf[c], ((0,), (0,)))
+
+    def merge(c):
+        @pl.when(c < NZ - 2)
+        def _():
+            zb_copy(c + 2).wait_recv()
+            zs_buf[c] = (share_buf[c] + zb_buf[c + 2].astype(F32)).astype(BF)
+
+        @pl.when(c >= NZ - 2)
+        def _():
+            zs_buf[c] = share_buf[c].astype(BF)
+
+        zb_copy(c).start()
+
+    stages = dict(
+        forward=forward, select=select, gather1=gather1, gather2=gather2, ffn=ffn,
+        scatter1=scatter1, scatter2=scatter2, unselect=unselect, merge=merge,
+    )
+    first_ffn = min(dict(SCHEDULE)["ffn"])
 
     def step(i, carry):
-        c3 = i - 2
-
-        @pl.when(on(c3))
-        def _():
-            for k in range(2):
-                a1_arrival(c3, k).wait_recv()
-                a2_copy(c3, k).start()
-
-        c2 = i - 1
-
-        @pl.when(on(c2))
-        def _():
-            for r in (1, 3, 2):
-                x_arrival(c2, r).wait_recv()
-            for k in range(2):
-                a1_copy(c2, k).start()
-            x_buf[c2, y] = xr_buf[c2, :, 0:CA]
-
-        c5 = i - 4
-
-        @pl.when(on(c5))
-        def _():
-            for k in range(2):
-                to = ym if k else yp
-                part = slice(k * half, (k + 1) * half)
-                r1_copy(c5, k).wait_recv()
-                p_buf[c5, to, part, 0:CA] = (
-                    p_buf[c5, to, part, 0:CA].astype(F32) + r1_buf[c5, k].astype(F32)
-                ).astype(BF)
-                r2_copy(c5, k).start()
-
-        c1 = i
-
-        @pl.when(on(c1))
-        def _():
-            @pl.when(c1 > 0)
-            def _():
-                for cp in z_copies(0, c1, at_z(z)):
-                    cp.wait_recv()
-
-            @pl.when(c1 < NZ - 2)
-            def _():
-                dz = jnp.where(c1 % 2 == 1, 1, NZ - 1)
-                for cp in z_copies(c1, c1 + 2, at_z((z + dz) % NZ)):
-                    cp.start()
-
-            route(c1)
-            for r in (1, 3, 2):
-                x_copy(c1, r).start()
-
-        c6 = i - 5
-
-        @pl.when(on(c6))
-        def _():
-            for k in range(2):
-                r2_copy(c6, k).wait_recv()
-            q_buf[c6, :, 0:CA] = (
-                p_buf[c6, y, :, 0:CA].astype(F32)
-                + r2_buf[c6, 0].astype(F32)
-                + r2_buf[c6, 1].astype(F32)
-            ).astype(BF)
-            for j in range(NT):
-                q_buf[c6, :, CA + CB * j : CA + CB * (j + 1)] = p_buf[c6, j, :, CA:SLICE]
-            for r in (1, 3, 2):
-                xb_copy(c6, r).start()
-            xb_buf[c6, rows48(x)] = q_buf[c6, rows48(x)]
-
-        c7 = i - 6
-
-        @pl.when(on(c7))
-        def _():
-            for r in (1, 3, 2):
-                xb_arrival(c7, r).wait_recv()
-            share = dot(sel[c7], xb_buf[c7], ((0,), (0,)))
-
-            @pl.when(c7 == 0)
-            def _():
-                acc[...] = share
-
-            @pl.when(c7 > 0)
-            def _():
-                zs_buf[c7] = share.astype(BF)
-                zb_copy(c7).start()
-
-        c8 = i - 7
-
-        @pl.when((c8 >= 1) & (c8 < NZ))
-        def _():
-            zb_copy(c8).wait_recv()
-            acc[...] += zb_buf[c8].astype(F32)
-
-        c4 = i - 3
-
-        @pl.when(c4 == 0)
+        @pl.when(i == first_ffn)
         def _():
             for load in loads:
                 load.wait()
 
-        @pl.when(on(c4))
-        def _():
-            for k in range(2):
-                a2_arrival(c4, k).wait_recv()
-            experts(c4)
-            for k in range(2):
-                r1_copy(c4, k).start()
+        for name, slots in SCHEDULE:
+            chunk = jnp.int32(-1)
+            for c, slot in enumerate(slots):
+                if slot >= 0:
+                    chunk = jnp.where(i == slot, c, chunk)
+
+            @pl.when(chunk >= 0)
+            def _(name=name, chunk=chunk):
+                stages[name](chunk)
 
         return carry
 
-    lax.fori_loop(0, NZ + 7, step, 0)
-
+    lax.fori_loop(0, SLOTS, step, 0)
+
+    for c in (1, 2):
+        zb_copy(c).wait_recv()
+    acc[...] = share_buf[0] + zb_buf[1].astype(F32) + zb_buf[2].astype(F32)
     for r in (1, 3, 2):
         bs_buf[r - 1] = acc[:, bcol((y + r) % NT)].astype(BF)
         bb_copy(r).start()
@@ -385,7 +397,6 @@
 
 
 def per_device(tokens, expert_ids, combine_weight, gate_weight, up_weight, down_weight):
-    meta = jnp.concatenate([expert_ids.astype(BF), combine_weight], axis=1).T
     flat = (HID, DM)
     vmem = pl.BlockSpec(memory_space=pltpu.VMEM)
     hbm = pl.BlockSpec(memory_space=pl.ANY)
@@ -393,7 +404,7 @@
     return pl.pallas_call(
         kernel,
         out_shape=jax.ShapeDtypeStruct((TOK, SLICE), BF),
-        in_specs=[vmem, vmem, hbm, hbm, hbm],
+        in_specs=[vmem, vmem, vmem, hbm, hbm, hbm],
         out_specs=vmem,
         scratch_shapes=[
             pltpu.VMEM(flat, BF), pltpu.VMEM(flat, BF), pltpu.VMEM(flat, BF),
@@ -411,13 +422,14 @@
             pltpu.VMEM((NZ, 2, ROWS, CA), BF),
             pltpu.VMEM((NZ, ROWS, TW), BF),
             pltpu.VMEM((NZ, ROWS, TW), BF),
+            pltpu.VMEM((NZ, TOK, TW), F32),
             pltpu.VMEM((NZ, TOK, TW), BF),
             pltpu.VMEM((NZ, TOK, TW), BF),
             pltpu.VMEM((TOK, TW), F32),
             pltpu.VMEM((NT - 1, TOK, CB), BF),
             pltpu.VMEM((NT - 1, TOK, CB), BF),
             dma((3,)),
-            dma((NZ,)), dma((NZ,)), dma((NZ,)), dma((NZ,)),
+            dma((NZ,)), dma((NZ,)), dma((NZ,)), dma((NZ,)), dma((NZ,)), dma((NZ,)),
             dma((NZ, 3)), dma((NZ, 3)),
             dma((NZ, 2)), dma((NZ, 2)), dma((NZ, 2)), dma((NZ, 2)),
             dma((NZ, 2)), dma((NZ, 2)), dma((NZ, 2)), dma((NZ, 2)),
@@ -430,7 +442,7 @@
         ),
         name="moe",
     )(
-        tokens, meta, gate_weight.reshape(flat), up_weight.reshape(flat), down_weight.reshape(flat)
+        tokens, expert_ids, combine_weight, gate_weight.reshape(flat), up_weight.reshape(flat), down_weight.reshape(flat)
     )
 
 

time: 141 us -> 122 us (0.87); the launches traced: 141 us -> 120 us
  Pallas kernels: 137 us -> 116 us
  local copies, waits for them, and re-layouts: 1.57 us -> 4.36 us
  other arithmetic: 1.96 us -> 0 us
    pallas_call x1, Pallas kernels: 137 us -> 116 us  [per_device(): pl.pallas_call(kernel, out_shape=jax.ShapeDtypeStruct((TOK, SLICE), BF),...]
    unnamed x1 -> x3, local copies, waits for them, and re-layouts: 1.57 us -> 4.36 us
where the time goes in v2:
time: 122 us; the launch traced here: 120 us
  Pallas kernels  116 us (95%)
  local copies, waits for them, and re-layouts  4.36 us (4%)
    pallas_call x1, Pallas kernels, per_device(): pl.pallas_call(kernel, out_shape=jax.ShapeDtypeStruct((TOK, SLICE), BF),...  116 us
    unnamed x3, local copies, waits for them, and re-layouts  4.36 us

profile of v2, /device:TPU:4, one launch (start us, length us, event | category | flops | bytes accessed | tf_op | source)
XLA Modules:
  0.0 120.0 jit_solution(4372651813737123712)
XLA Ops:
  0.0 1.4 %copy.8.comb_ref = bf16[128,8]{1,0:T(8,128)(2,1)} copy(bf16[128,8]{0,1:T(8,128)(2,1)} %param.8) | data formatting | bytes 4096 | tf_op args[2]
  1.4 1.4 %copy.7.ids_ref = s32[128,8]{1,0:T(8,128)} copy(s32[128,8]{0,1:T(8,128)} %param.7) | data formatting | bytes 8192 | tf_op args[1]
  2.8 115.6 %moe.1 = bf16[128,512]{1,0:T(8,128)(2,1)} custom-call(bf16[128,512]{1,0:T(8,128)(2,1)} %tok_ref.1, s32[128,8]{1,0:T(8,128)} %copy.7.ids_ref, bf16[128,8]{1,0:T(8,128)(2,1)} %copy.8.comb_ref, bf16[768,2048]{1,0:T(8,128)(2,1)} %bitcast.3, bf16[768,2048]{1,0:T(8,128)(2,1)} %bitcast.4, bf16[768,2048]{1,0:T(8,128)(2,1)} %bitcast.5), custom_call_target="tpu_custom_call" | custom-call | tf_op jit(solution)/shard_map/moe/pallas_call | solution.py:404
  118.4 1.6 %copy.10 = bf16[128,512]{1,0:T(8,128)(2,1)} copy(bf16[128,512]{1,0:T(8,128)(2,1)} %moe.1) | data formatting | bytes 262144

commit v3 on v0

v3 whole, which is shorter than its diff:
```python
import jax
import jax.numpy as jnp
from jax import lax
from jax.experimental import pallas as pl
from jax.experimental.pallas import tpu as pltpu
from jax.sharding import PartitionSpec as P

NT = 4
NX = 4
NZ = 8
TOK = 128
CAP = 48
ROWS = NX * CAP
HALF = ROWS // 2
SLICE = 512
AD = 256
AR = 384
BD = SLICE - AD
BR = SLICE - AR
HID = 768
DM = NT * SLICE
BF = jnp.bfloat16
F32 = jnp.float32

SLOTS = 47
SCHEDULE = (
    ("scatter2", (40, 35, 42, 34, 32, 30, 27, 29)),
    ("forward_b", (2, 7, 6, 10, 11, 16, -1, -1)),
    ("select_a", (0, 4, 3, 7, 5, 8, 11, 14)),
    ("gather2", (7, 9, 20, 14, 11, 15, 17, 19)),
    ("return_b", (35, 26, 31, 20, 25, 24, 21, 22)),
    ("merge_a", (-1, 45, 46, 42, 43, 37, 38, 31)),
    ("gather1", (5, 7, 16, 9, 8, 13, 14, 17)),
    ("unselect_b", (46, 36, 38, 22, 31, 28, 23, 27)),
    ("select_b", (2, 7, 21, 12, 11, 16, 15, 18)),
    ("merge_b", (-1, 38, 39, 33, 32, 30, 23, 27)),
    ("finish_b", (46, -1, -1, -1, -1, -1, -1, -1)),
    ("forward_a", (-1, 1, 0, 5, 3, 7, -1, -1)),
    ("scatter1", (31, 29, 35, 27, 18, 22, 21, 26)),
    ("ffn", (27, 13, 30, 17, 16, 20, 18, 21)),
    ("unselect_a", (46, 43, 44, 40, 41, 34, 36, 30)),
)


def dot(a, b, dims=((1,), (0,))):
    return lax.dot_general(a, b, (dims, ((), ())), preferred_element_type=F32)


def iota(shape, dim):
    return lax.broadcasted_iota(jnp.int32, shape, dim)


def kernel(
    tok_hbm, ids_hbm, comb_hbm, gate_hbm, up_hbm, down_hbm, out_hbm,
    wg, wu, wd, expand, ids_v, comb_v, ta, tb, meta, sel, xsa, xsb, xrb, wts, wtr, xin, x_all, hid,
    pa, pb, r1, r2, qa, xba, xbb, sha, shb, zsa, zsb, zra, zrb, bs, br, outv,
    w_sem, in_sem, out_sem, m_s, m_r, za_s, za_r, zb_s, zb_r, xa_s, xa_r, xw_s, xw_r, xb_s, xb_r,
    g1_s, g1_r, g2_s, g2_r, s1_s, s1_r, s2_s, s2_r, ya_s, ya_r, yb_s, yb_r, ca_s, ca_r, cb_s, cb_r,
    b_s, b_r, bb_s, bb_r,
):
    y = lax.axis_index("tensor")
    e = lax.axis_index("expert")
    z = e // NX
    x = e % NX
    yp = (y + 1) % NT
    yo = (y + 2) % NT
    ym = (y + 3) % NT

    def at_y(j):
        return {"tensor": j}

    def at_x(j):
        return {"expert": z * NX + j}

    def at_z(j):
        return {"expert": (j % NZ) * NX + x}

    def rcopy(src, dst, ssem, rsem, dev):
        return pltpu.make_async_remote_copy(
            src_ref=src, dst_ref=dst, send_sem=ssem, recv_sem=rsem,
            device_id=dev, device_id_type=pl.DeviceIdType.MESH,
        )

    def rows48(j):
        return pl.ds(pl.multiple_of(j * CAP, 16), CAP)

    def bcol(j, width):
        return pl.ds(pl.multiple_of(width * j, 128), width)

    def m_copy(src, slot, dev):
        return rcopy(meta.at[src], meta.at[slot], m_s.at[slot], m_r.at[slot], dev)

    def za_copy(src, slot, dev):
        return rcopy(ta.at[src], ta.at[slot], za_s.at[slot], za_r.at[slot], dev)

    def zb_copy(src, slot, dev):
        return rcopy(tb.at[src], tb.at[slot], zb_s.at[slot], zb_r.at[slot], dev)

    def xa_copy(c, r, frm, to):
        return rcopy(
            xsa.at[c, rows48(to)], xin.at[c, y, rows48(frm)],
            xa_s.at[c, r - 1], xa_r.at[c, r - 1], at_x(to),
        )

    def xw_copy(c, r, frm, to):
        return rcopy(wts.at[c, to], wtr.at[c, frm], xw_s.at[c, r - 1], xw_r.at[c, r - 1], at_x(to))

    def xb_copy(c, r, frm, to):
        return rcopy(
            xsb.at[c, rows48(to)], xrb.at[c, rows48(frm)],
            xb_s.at[c, r - 1], xb_r.at[c, r - 1], at_x(to),
        )

    def ya_copy(c, r, frm, to):
        return rcopy(
            qa.at[c, rows48(to)], xba.at[c, rows48(frm)],
            ya_s.at[c, r - 1], ya_r.at[c, r - 1], at_x(to),
        )

    def yb_copy(c, r, frm, to):
        return rcopy(
            pb.at[c, rows48(to)], xbb.at[c, rows48(frm)],
            yb_s.at[c, r - 1], yb_r.at[c, r - 1], at_x(to),
        )

    def to_x(copy, c, r):
        return copy(c, r, x, (x + r) % NX)

    def from_x(copy, c, r):
        frm = (x + NX - r) % NX
        return copy(c, r, frm, frm)

    def g1_copy(c, k):
        return rcopy(xin.at[c, y], xin.at[c, y], g1_s.at[c, k], g1_r.at[c, k], at_y(ym if k else yp))

    def g1_arrival(c, k):
        frm = yp if k else ym
        return rcopy(xin.at[c, frm], xin.at[c, frm], g1_s.at[c, k], g1_r.at[c, k], at_y(frm))

    def g2_copy(c, k):
        blk = xin.at[c, yp if k else ym, pl.ds(k * HALF, HALF)]
        return rcopy(blk, blk, g2_s.at[c, k], g2_r.at[c, k], at_y(ym if k else yp))

    def g2_arrival(c, k):
        blk = xin.at[c, yo, pl.ds(k * HALF, HALF)]
        return rcopy(blk, blk, g2_s.at[c, k], g2_r.at[c, k], at_y(yp if k else ym))

    def s1_copy(c, k):
        return rcopy(
            pa.at[c, yo, pl.ds(k * HALF, HALF)], r1.at[c, k],
            s1_s.at[c, k], s1_r.at[c, k], at_y(ym if k else yp),
        )

    def s2_copy(c, k):
        to = ym if k else yp
        return rcopy(pa.at[c, to], r2.at[c, k], s2_s.at[c, k], s2_r.at[c, k], at_y(to))

    def home(c):
        return at_z(jnp.where(c % 2 == 1, z + NZ - 1, z + 1))

    def ca_copy(c):
        return rcopy(zsa.at[c], zra.at[c], ca_s.at[c], ca_r.at[c], home(c))

    def cb_copy(c):
        return rcopy(zsb.at[c], zrb.at[c], cb_s.at[c], cb_r.at[c], home(c))

    def b_copy(r):
        blk = tb.at[0, :, bcol(y, BD)]
        return rcopy(blk, blk, b_s.at[r - 1], b_r.at[r - 1], at_y((y + r) % NT))

    def b_arrival(r):
        frm = (y + NT - r) % NT
        blk = tb.at[0, :, bcol(frm, BD)]
        return rcopy(blk, blk, b_s.at[r - 1], b_r.at[r - 1], at_y(frm))

    def bb_copy(r):
        return rcopy(bs.at[r - 1], br.at[r - 1], bb_s.at[r - 1], bb_r.at[r - 1], at_y((y + r) % NT))

    near = (1, 3, 2)

    inputs = [
        pltpu.make_async_copy(src, dst, in_sem.at[k])
        for k, (src, dst) in enumerate((
            (tok_hbm.at[:, pl.ds(AD, BD)], tb.at[0, :, bcol(y, BD)]),
            (ids_hbm, ids_v),
            (comb_hbm, comb_v),
            (tok_hbm.at[:, pl.ds(0, AD)], ta.at[0]),
        ))
    ]
    loads = [
        pltpu.make_async_copy(src, dst, w_sem.at[k])
        for k, (src, dst) in enumerate(((gate_hbm, wg), (up_hbm, wu), (down_hbm, wd)))
    ]
    for load in inputs:
        load.start()

    barrier = pltpu.get_barrier_semaphore()
    peers = [at_y((y + r) % NT) for r in range(1, NT)]
    peers += [at_x((x + r) % NX) for r in range(1, NX)]
    peers += [at_z(z + r) for r in (1, NZ - 1)]
    for peer in peers:
        pl.semaphore_signal(barrier, 1, device_id=peer, device_id_type=pl.DeviceIdType.MESH)
    for load in loads:
        load.start()

    base = (iota((16, HID), 0) - NX * x) * (HID // NX)
    hid_n = iota((16, HID), 1)
    expand[...] = jnp.where((hid_n >= base) & (hid_n < base + HID // NX), 1.0, 0.0).astype(BF)
    for load in inputs:
        load.wait()
    meta[0] = jnp.concatenate([ids_v[...].astype(F32), comb_v[...].astype(F32)], axis=0).astype(BF)

    pl.semaphore_wait(barrier, len(peers))
    for r in near:
        b_copy(r).start()
    for copy in (za_copy, m_copy):
        for slot, dz in ((1, 1), (2, NZ - 1)):
            copy(0, slot, at_z(z + dz)).start()

    def forward_a(c):
        for copy in (m_copy, za_copy):
            copy(0, c, at_z(z)).wait_recv()
        for copy in (m_copy, za_copy):
            copy(c, c + 2, at_z(z + jnp.where(c % 2 == 1, 1, NZ - 1))).start()

    def forward_b(c):
        @pl.when(c == 0)
        def _():
            for r in near:
                b_arrival(r).wait_recv()
            zb_copy(0, 1, at_z(z + 1)).start()
            zb_copy(0, 2, at_z(z + NZ - 1)).start()

        @pl.when(c > 0)
        def _():
            zb_copy(0, c, at_z(z)).wait_recv()
            zb_copy(c, c + 2, at_z(z + jnp.where(c % 2 == 1, 1, NZ - 1))).start()

    def select_a(c):
        @pl.when(c >= NZ - 2)
        def _():
            for copy in (m_copy, za_copy):
                copy(0, c, at_z(z)).wait_recv()

        info = meta[c].astype(F32)
        rel = info[0:8] - jnp.asarray(NX * NX * z, F32)
        comb = info[8:16]
        sub16 = iota((16, TOK), 0)
        present = jnp.zeros((16, TOK), F32)
        rows = []
        for xx in range(NX):
            inside = (rel >= float(NX * xx)) & (rel < float(NX * xx + NX))
            row = jnp.max(jnp.where(inside, 1.0, 0.0), axis=0, keepdims=True)
            rows.append(row)
            present = jnp.where(sub16 == xx, row, present)
        earlier = jnp.where(iota((TOK, TOK), 0) < iota((TOK, TOK), 1), 1.0, 0.0).astype(BF)
        before = dot(present.astype(BF), earlier)
        slot = iota((CAP, TOK), 0).astype(F32)
        wide = jnp.zeros((16, TOK), F32)
        for i in range(8):
            wide = jnp.where(sub16.astype(F32) == rel[i : i + 1], comb[i : i + 1], wide)
        wide = wide.astype(BF)
        for xx in range(NX):
            hit = (slot == before[xx : xx + 1]) & (rows[xx] > 0.5)
            block = jnp.where(hit, 1.0, 0.0).astype(BF)
            sel[c, xx * CAP : (xx + 1) * CAP] = block
            wts[c, xx, :, 0:CAP] = dot(wide, block, ((1,), (1,))).astype(BF)
        xsa[c] = dot(sel[c], ta[c]).astype(BF)
        xin[c, y, rows48(x)] = xsa[c, rows48(x)]
        wtr[c, x, :, 0:CAP] = wts[c, x, :, 0:CAP]
        for r in near:
            to_x(xa_copy, c, r).start()
        for r in near:
            to_x(xw_copy, c, r).start()

    def select_b(c):
        @pl.when(c >= NZ - 2)
        def _():
            zb_copy(0, c, at_z(z)).wait_recv()

        xsb[c] = dot(sel[c], tb[c]).astype(BF)
        xrb[c, rows48(x)] = xsb[c, rows48(x)]
        for r in near:
            to_x(xb_copy, c, r).start()

    def gather1(c):
        for r in near:
            from_x(xa_copy, c, r).wait_recv()
        for k in range(2):
            g1_copy(c, k).start()

    def gather2(c):
        for k in range(2):
            g1_arrival(c, k).wait_recv()
            g2_copy(c, k).start()

    def ffn(c):
        for r in near:
            from_x(xw_copy, c, r).wait_recv()
            from_x(xb_copy, c, r).wait_recv()
        for k in range(2):
            g2_arrival(c, k).wait_recv()
        for j in range(NT):
            x_all[:, j * SLICE : j * SLICE + AD] = xin[c, j]
            x_all[:, j * SLICE + AD : (j + 1) * SLICE] = xrb[c, :, BD * j : BD * (j + 1)]
        rows_in = x_all[...]
        for n in range(HID // 256):
            cols = slice(n * 256, (n + 1) * 256)
            gate = dot(rows_in, wg[cols], ((1,), (1,)))
            up = dot(rows_in, wu[cols], ((1,), (1,)))
            scale = jnp.concatenate(
                [dot(wtr[c, xx, :, 0:CAP], expand[:, cols], ((0,), (0,))) for xx in range(NX)], axis=0
            )
            hid[:, cols] = (gate / (1.0 + jnp.exp(-gate)) * up * scale).astype(BF)
        h = hid[...]
        for j in range(NT):
            for n in range(SLICE // 256):
                lo = n * 256
                part = dot(h, wd[:, j * SLICE + lo : j * SLICE + lo + 256]).astype(BF)
                split = min(max(AR - lo, 0), 256)
                if split:
                    pa[c, j, :, lo : lo + split] = part[:, :split]
                if split < 256:
                    at = BR * j + lo + split - AR
                    pb[c, :, at : at + 256 - split] = part[:, split:]
        for k in range(2):
            s1_copy(c, k).start()

    def scatter1(c):
        for k in range(2):
            to = ym if k else yp
            part = slice(k * HALF, (k + 1) * HALF)
            s1_copy(c, k).wait_recv()
            pa[c, to, part] = (pa[c, to, part].astype(F32) + r1[c, k].astype(F32)).astype(BF)
            s2_copy(c, k).start()

    def scatter2(c):
        for k in range(2):
            s2_copy(c, k).wait_recv()
        qa[c] = (pa[c, y].astype(F32) + r2[c, 0].astype(F32) + r2[c, 1].astype(F32)).astype(BF)
        for r in near:
            to_x(ya_copy, c, r).start()
        xba[c, rows48(x)] = qa[c, rows48(x)]

    def return_b(c):
        for r in near:
            to_x(yb_copy, c, r).start()
        xbb[c, rows48(x)] = pb[c, rows48(x)]

    def unselect_a(c):
        for r in near:
            from_x(ya_copy, c, r).wait_recv()
        sha[c] = dot(sel[c], xba[c], ((0,), (0,)))

    def unselect_b(c):
        for r in near:
            from_x(yb_copy, c, r).wait_recv()
        shb[c] = dot(sel[c], xbb[c], ((0,), (0,)))

    def merge(c, copy, share, out, arrived):
        @pl.when(c < NZ - 2)
        def _():
            copy(c + 2).wait_recv()
            out[c] = (share[c] + arrived[c + 2].astype(F32)).astype(BF)

        @pl.when(c >= NZ - 2)
        def _():
            out[c] = share[c].astype(BF)

        copy(c).start()

    def merge_a(c):
        merge(c, ca_copy, sha, zsa, zra)

    def merge_b(c):
        merge(c, cb_copy, shb, zsb, zrb)

    def finish_b(c):
        for k in (1, 2):
            cb_copy(k).wait_recv()
        shb[0] += zrb[1].astype(F32) + zrb[2].astype(F32)
        for r in near:
            bs[r - 1] = shb[0, :, bcol((y + r) % NT, BR)].astype(BF)
            bb_copy(r).start()

    stages = dict(
        forward_a=forward_a, forward_b=forward_b, select_a=select_a, select_b=select_b,
        gather1=gather1, gather2=gather2, ffn=ffn, scatter1=scatter1, scatter2=scatter2,
        return_b=return_b, unselect_a=unselect_a, unselect_b=unselect_b,
        merge_a=merge_a, merge_b=merge_b, finish_b=finish_b,
    )
    first_ffn = min(dict(SCHEDULE)["ffn"])

    def step(i, carry):
        @pl.when(i == first_ffn)
        def _():
            for load in loads:
                load.wait()

        for name, slots in SCHEDULE:
            chunk = jnp.int32(-1)
            for c, slot in enumerate(slots):
                if slot >= 0:
                    chunk = jnp.where(i == slot, c, chunk)

            @pl.when(chunk >= 0)
            def _(name=name, chunk=chunk):
                stages[name](chunk)

        return carry

    lax.fori_loop(0, SLOTS, step, 0)

    total = shb[0, :, bcol(y, BR)]
    for r in near:
        bb_copy(r).wait_recv()
        total = total + br[r - 1].astype(F32)
    outv[:, AR:SLICE] = total.astype(BF)
    for c in (1, 2):
        ca_copy(c).wait_recv()
    outv[:, 0:AR] = (sha[0] + zra[1].astype(F32) + zra[2].astype(F32)).astype(BF)
    result = pltpu.make_async_copy(outv, out_hbm, out_sem)
    result.start()

    def drain(c, carry):
        for k in range(2):
            for cp in (g1_copy, g2_copy, s1_copy, s2_copy):
                cp(c, k).wait_send()
        for r in near:
            for cp in (xa_copy, xw_copy, xb_copy, ya_copy, yb_copy):
                to_x(cp, c, r).wait_send()

        @pl.when(c > 0)
        def _():
            for copy in (m_copy, za_copy, zb_copy):
                copy(0, c, at_z(z)).wait_send()
            ca_copy(c).wait_send()
            cb_copy(c).wait_send()

        return carry

    lax.fori_loop(0, NZ, drain, 0)
    for r in near:
        b_copy(r).wait_send()
        bb_copy(r).wait_send()
    result.wait()


def per_device(tokens, expert_ids, combine_weight, gate_weight, up_weight, down_weight):
    flat = (HID, DM)
    hbm = pl.BlockSpec(memory_space=pl.ANY)
    dma = pltpu.SemaphoreType.DMA

    def vmem(*shape, dtype=BF):
        return pltpu.VMEM(shape, dtype)

    return pl.pallas_call(
        kernel,
        out_shape=jax.ShapeDtypeStruct((TOK, SLICE), BF),
        in_specs=[hbm] * 6,
        out_specs=hbm,
        scratch_shapes=[
            vmem(*flat), vmem(*flat), vmem(*flat),
            vmem(16, HID), vmem(8, TOK, dtype=jnp.int32), vmem(8, TOK),
            vmem(NZ, TOK, AD), vmem(NZ, TOK, NT * BD), vmem(NZ, 16, TOK), vmem(NZ, ROWS, TOK),
            vmem(NZ, ROWS, AD), vmem(NZ, ROWS, NT * BD), vmem(NZ, ROWS, NT * BD),
            vmem(NZ, NX, 16, 128), vmem(NZ, NX, 16, 128),
            vmem(NZ, NT, ROWS, AD), vmem(ROWS, DM), vmem(ROWS, HID),
            vmem(NZ, NT, ROWS, AR), vmem(NZ, ROWS, NT * BR),
            vmem(NZ, 2, HALF, AR), vmem(NZ, 2, ROWS, AR), vmem(NZ, ROWS, AR),
            vmem(NZ, ROWS, AR), vmem(NZ, ROWS, NT * BR),
            vmem(NZ, TOK, AR, dtype=F32), vmem(NZ, TOK, NT * BR, dtype=F32),
            vmem(NZ, TOK, AR), vmem(NZ, TOK, NT * BR),
            vmem(NZ, TOK, AR), vmem(NZ, TOK, NT * BR),
            vmem(NT - 1, TOK, BR), vmem(NT - 1, TOK, BR), vmem(TOK, SLICE),
            dma((3,)), dma((4,)), dma,
            *[dma((NZ,))] * 6,
            *[dma((NZ, 3))] * 6,
            *[dma((NZ, 2))] * 8,
            *[dma((NZ, 3))] * 4,
            *[dma((NZ,))] * 4,
            *[dma((3,))] * 4,
        ],
        compiler_params=pltpu.CompilerParams(
            collective_id=0, has_side_effects=True, vmem_limit_bytes=60 * 2**20
        ),
        name="moe",
    )(
        tokens, expert_ids.T, combine_weight.T,
        gate_weight.reshape(flat), up_weight.reshape(flat), down_weight.reshape(flat),
    )


def solution(mesh):
    in_specs = (
        P(("dp", "expert"), "tensor"),
        P(("dp", "expert"), None),
        P(("dp", "expert"), None),
        P("expert", "tensor", None),
        P("expert", "tensor", None),
        P("expert", "tensor", None),
    )
    out_specs = P(("dp", "expert"), "tensor")
    return jax.shard_map(
        per_device, mesh=mesh, in_specs=in_specs, out_specs=out_specs, check_vma=False
    )
```

time: 457 us -> 101 us (0.22); the launches traced: 450 us -> 101 us
  other arithmetic: 117 us -> 0 us
  local copies, waits for them, and re-layouts: 102 us -> 1.57 us
  Pallas kernels: 0 us -> 98.9 us
  waiting for transfers between devices: 96 us -> 0 us
  blocking collectives: 63.9 us -> 0 us
  matrix products: 45.3 us -> 0 us
  between operations: 14.3 us -> 0.01 us
  starting transfers between devices: 10.2 us -> 0 us
    scatter-add x5 -> x0, other arithmetic: 105 us -> none  [the longest x4 95.5 us: per_device(): combined.at[source].add(row_weight[:, None] * expert_out, mode='drop')]
    pallas_call x0 -> x1, Pallas kernels: none -> 98.9 us  [per_device(): pl.pallas_call(kernel, out_shape=jax.ShapeDtypeStruct((TOK, SLICE), BF),...]
    reduce_scatter x1 -> x0, waiting for transfers between devices: 67.4 us -> none  [per_device(): lax.psum_scatter(combined.astype(jnp.bfloat16), 'tensor', scatter_dimensi...]
    all_to_all x2 -> x0, blocking collectives: 63.9 us -> none  [the longest x1 50.8 us: per_device(): lax.all_to_all(outgoing, 'expert', split_axis=0, concat_axis=0, tiled=True)]
    gather x8 -> x0, local copies, waits for them, and re-layouts: 60.3 us -> none  [the longest x4 42.5 us: per_device(): rows_in = flat_rows[safe_source]]
    dot_general x10 -> x0, matrix products: 45.3 us -> none  [the longest x4 29.4 us: per_device(): jnp.dot(hidden, down_weight[expert_slot], preferred_element_type=jnp.floa...]
    scatter x5 -> x0, local copies, waits for them, and re-layouts: 40.4 us -> none  [the longest x4 24.9 us: per_device(): jnp.full((expert_cap,), row_total, jnp.int32).at[target]]
    all_to_all x1 -> x0, waiting for transfers between devices: 23.5 us -> none  [per_device(): lax.all_to_all(summed.astype(jnp.bfloat16), 'expert', split_axis=0, conca...]
  transfers between devices with their start and end apart: 3 -> 0, of which waited for: 3 -> 0; matrix products, arithmetic and copies ran while one was open for 14% -> 0% of each run, Pallas kernels for 0% -> 0%
where the time goes in v3:
time: 101 us
  Pallas kernels  98.9 us (98%)
  local copies, waits for them, and re-layouts  1.57 us (2%)
    pallas_call x1, Pallas kernels, per_device(): pl.pallas_call(kernel, out_shape=jax.ShapeDtypeStruct((TOK, SLICE), BF),...  98.9 us

profile of v3, /device:TPU:4, one launch (start us, length us, event | category | flops | bytes accessed | tf_op | source)
XLA Modules:
  0.0 100.5 jit_solution(11798574082464700805)
XLA Ops:
  0.0 98.9 %moe.1 = bf16[128,512]{1,0:T(8,128)(2,1)} custom-call(bf16[128,512]{1,0:T(8,128)(2,1)} %tok_hbm.1, s32[8,128]{1,0:T(8,128)} %bitcast.8, bf16[8,128]{1,0:T(8,128)(2,1)} %bitcast.9, bf16[768,2048]{1,0:T(8,128)(2,1)} %bitcast.5, bf16[768,2048]{1,0:T(8,128)(2,1)} %bitcast.6, bf16[768,2048]{1,0:T(8,128)(2,1)} %bitcast.7), custom_call_target="tpu_custom_call" | custom-call | tf_op jit(solution)/shard_map/moe/pallas_call | solution.py:457
  98.9 1.6 %copy.8 = bf16[128,512]{1,0:T(8,128)(2,1)} copy(bf16[128,512]{1,0:T(8,128)(2,1)} %moe.1) | data formatting | bytes 262144

commit v4 on v3

--- a/solution.py
+++ b/solution.py
@@ -22,23 +22,23 @@
 BF = jnp.bfloat16
 F32 = jnp.float32
 
-SLOTS = 47
+SLOTS = 45
 SCHEDULE = (
-    ("scatter2", (40, 35, 42, 34, 32, 30, 27, 29)),
-    ("forward_b", (2, 7, 6, 10, 11, 16, -1, -1)),
-    ("select_a", (0, 4, 3, 7, 5, 8, 11, 14)),
-    ("gather2", (7, 9, 20, 14, 11, 15, 17, 19)),
-    ("return_b", (35, 26, 31, 20, 25, 24, 21, 22)),
-    ("merge_a", (-1, 45, 46, 42, 43, 37, 38, 31)),
-    ("gather1", (5, 7, 16, 9, 8, 13, 14, 17)),
-    ("unselect_b", (46, 36, 38, 22, 31, 28, 23, 27)),
-    ("select_b", (2, 7, 21, 12, 11, 16, 15, 18)),
-    ("merge_b", (-1, 38, 39, 33, 32, 30, 23, 27)),
-    ("finish_b", (46, -1, -1, -1, -1, -1, -1, -1)),
-    ("forward_a", (-1, 1, 0, 5, 3, 7, -1, -1)),
-    ("scatter1", (31, 29, 35, 27, 18, 22, 21, 26)),
-    ("ffn", (27, 13, 30, 17, 16, 20, 18, 21)),
-    ("unselect_a", (46, 43, 44, 40, 41, 34, 36, 30)),
+    ("scatter1", (39, 20, 31, 33, 21, 24, 27, 26)),
+    ("select_a", (0, 1, 2, 6, 7, 11, 10, 15)),
+    ("forward_a", (-1, 0, 1, 4, 6, 9, -1, -1)),
+    ("gather2", (5, 9, 11, 15, 16, 18, 17, 20)),
+    ("forward_b", (1, 7, 8, 12, 13, 18, -1, -1)),
+    ("select_b", (3, 7, 11, 21, 16, 18, 19, 20)),
+    ("return_b", (41, 34, 25, 30, 26, 21, 24, 23)),
+    ("scatter2", (44, 23, 39, 38, 36, 32, 31, 29)),
+    ("merge_a", (-1, 28, 44, 43, 42, 38, 37, 34)),
+    ("unselect_b", (44, 40, 34, 35, 33, 24, 29, 27)),
+    ("gather1", (2, 3, 4, 9, 11, 14, 13, 17)),
+    ("merge_b", (-1, 40, 39, 35, 34, 30, 29, 27)),
+    ("ffn", (11, 16, 18, 27, 19, 20, 21, 22)),
+    ("finish_b", (44, -1, -1, -1, -1, -1, -1, -1)),
+    ("unselect_a", (44, 27, 43, 42, 41, 37, 36, 33)),
 )
 
 
@@ -155,14 +155,15 @@
         to = ym if k else yp
         return rcopy(pa.at[c, to], r2.at[c, k], s2_s.at[c, k], s2_r.at[c, k], at_y(to))
 
-    def home(c):
-        return at_z(jnp.where(c % 2 == 1, z + NZ - 1, z + 1))
+    def homeward(c, hops):
+        return at_z(jnp.where(c % 2 == 1, z + NZ - hops, z + hops))
 
     def ca_copy(c):
-        return rcopy(zsa.at[c], zra.at[c], ca_s.at[c], ca_r.at[c], home(c))
+        hops = jnp.where((c + 1) // 2 == 2, 2, 1)
+        return rcopy(zsa.at[c], zra.at[c], ca_s.at[c], ca_r.at[c], homeward(c, hops))
 
     def cb_copy(c):
-        return rcopy(zsb.at[c], zrb.at[c], cb_s.at[c], cb_r.at[c], home(c))
+        return rcopy(zsb.at[c], zrb.at[c], cb_s.at[c], cb_r.at[c], homeward(c, 1))
 
     def b_copy(r):
         blk = tb.at[0, :, bcol(y, BD)]
@@ -197,7 +198,7 @@
     barrier = pltpu.get_barrier_semaphore()
     peers = [at_y((y + r) % NT) for r in range(1, NT)]
     peers += [at_x((x + r) % NX) for r in range(1, NX)]
-    peers += [at_z(z + r) for r in (1, NZ - 1)]
+    peers += [at_z(z + r) for r in (1, NZ - 1, 2, NZ - 2)]
     for peer in peers:
         pl.semaphore_signal(barrier, 1, device_id=peer, device_id_type=pl.DeviceIdType.MESH)
     for load in loads:
@@ -357,23 +358,23 @@
             from_x(yb_copy, c, r).wait_recv()
         shb[c] = dot(sel[c], xbb[c], ((0,), (0,)))
 
-    def merge(c, copy, share, out, arrived):
-        @pl.when(c < NZ - 2)
+    def merge(c, joins, copy, share, out, arrived):
+        @pl.when(joins)
         def _():
             copy(c + 2).wait_recv()
             out[c] = (share[c] + arrived[c + 2].astype(F32)).astype(BF)
 
-        @pl.when(c >= NZ - 2)
+        @pl.when(jnp.logical_not(joins))
         def _():
             out[c] = share[c].astype(BF)
 
         copy(c).start()
 
     def merge_a(c):
-        merge(c, ca_copy, sha, zsa, zra)
+        merge(c, (c >= 3) & (c < NZ - 2), ca_copy, sha, zsa, zra)
 
     def merge_b(c):
-        merge(c, cb_copy, shb, zsb, zrb)
+        merge(c, c < NZ - 2, cb_copy, shb, zsb, zrb)
 
     def finish_b(c):
         for k in (1, 2):
@@ -416,9 +417,11 @@
         bb_copy(r).wait_recv()
         total = total + br[r - 1].astype(F32)
     outv[:, AR:SLICE] = total.astype(BF)
-    for c in (1, 2):
+    total = sha[0]
+    for c in (4, 3, 2, 1):
         ca_copy(c).wait_recv()
-    outv[:, 0:AR] = (sha[0] + zra[1].astype(F32) + zra[2].astype(F32)).astype(BF)
+        total = total + zra[c].astype(F32)
+    outv[:, 0:AR] = total.astype(BF)
     result = pltpu.make_async_copy(outv, out_hbm, out_sem)
     result.start()
 

time: 101 us -> 96.8 us (0.958)
  Pallas kernels: 98.9 us -> 95.1 us
    pallas_call x1, Pallas kernels: 98.9 us -> 95.1 us  [per_device(): pl.pallas_call(kernel, out_shape=jax.ShapeDtypeStruct((TOK, SLICE), BF),...]
where the time goes in v4:
time: 96.8 us; the launch traced here: 96.7 us
  Pallas kernels  95.1 us (98%)
  local copies, waits for them, and re-layouts  1.57 us (2%)
    pallas_call x1, Pallas kernels, per_device(): pl.pallas_call(kernel, out_shape=jax.ShapeDtypeStruct((TOK, SLICE), BF),...  95.1 us

profile of v4, /device:TPU:4, one launch (start us, length us, event | category | flops | bytes accessed | tf_op | source)
XLA Modules:
  0.0 96.7 jit_solution(17718040888507621892)
XLA Ops:
  0.0 95.1 %moe.1 = bf16[128,512]{1,0:T(8,128)(2,1)} custom-call(bf16[128,512]{1,0:T(8,128)(2,1)} %tok_hbm.1, s32[8,128]{1,0:T(8,128)} %bitcast.8, bf16[8,128]{1,0:T(8,128)(2,1)} %bitcast.9, bf16[768,2048]{1,0:T(8,128)(2,1)} %bitcast.5, bf16[768,2048]{1,0:T(8,128)(2,1)} %bitcast.6, bf16[768,2048]{1,0:T(8,128)(2,1)} %bitcast.7), custom_call_target="tpu_custom_call" | custom-call | tf_op jit(solution)/shard_map/moe/pallas_call | solution.py:460
  95.1 1.6 %copy.8 = bf16[128,512]{1,0:T(8,128)(2,1)} copy(bf16[128,512]{1,0:T(8,128)(2,1)} %moe.1) | data formatting | bytes 262144

commit v5 on v4

--- a/solution.py
+++ b/solution.py
@@ -24,21 +24,21 @@
 
 SLOTS = 45
 SCHEDULE = (
-    ("scatter1", (39, 20, 31, 33, 21, 24, 27, 26)),
+    ("scatter2", (44, 24, 40, 39, 37, 33, 32, 29)),
+    ("merge_a", (-1, 28, 44, 43, 42, 39, 38, 35)),
     ("select_a", (0, 1, 2, 6, 7, 11, 10, 15)),
     ("forward_a", (-1, 0, 1, 4, 6, 9, -1, -1)),
+    ("scatter1", (39, 20, 31, 33, 21, 24, 27, 26)),
     ("gather2", (5, 9, 11, 15, 16, 18, 17, 20)),
+    ("unselect_b", (44, 41, 35, 36, 33, 25, 29, 27)),
     ("forward_b", (1, 7, 8, 12, 13, 18, -1, -1)),
+    ("finish_b", (44, -1, -1, -1, -1, -1, -1, -1)),
     ("select_b", (3, 7, 11, 21, 16, 18, 19, 20)),
-    ("return_b", (41, 34, 25, 30, 26, 21, 24, 23)),
-    ("scatter2", (44, 23, 39, 38, 36, 32, 31, 29)),
-    ("merge_a", (-1, 28, 44, 43, 42, 38, 37, 34)),
-    ("unselect_b", (44, 40, 34, 35, 33, 24, 29, 27)),
     ("gather1", (2, 3, 4, 9, 11, 14, 13, 17)),
-    ("merge_b", (-1, 40, 39, 35, 34, 30, 29, 27)),
-    ("ffn", (11, 16, 18, 27, 19, 20, 21, 22)),
-    ("finish_b", (44, -1, -1, -1, -1, -1, -1, -1)),
-    ("unselect_a", (44, 27, 43, 42, 41, 37, 36, 33)),
+    ("merge_b", (-1, 41, 40, 36, 35, 30, 29, 27)),
+    ("ffn", (11, 16, 18, 27, 19, 20, 22, 23)),
+    ("return_b", (41, 34, 25, 29, 26, 21, 24, 23)),
+    ("unselect_a", (44, 27, 43, 42, 41, 38, 37, 33)),
 )
 
 
@@ -177,7 +177,7 @@
     def bb_copy(r):
         return rcopy(bs.at[r - 1], br.at[r - 1], bb_s.at[r - 1], bb_r.at[r - 1], at_y((y + r) % NT))
 
-    near = (1, 3, 2)
+    near = (2, 1, 3)
 
     inputs = [
         pltpu.make_async_copy(src, dst, in_sem.at[k])
@@ -211,38 +211,7 @@
         load.wait()
     meta[0] = jnp.concatenate([ids_v[...].astype(F32), comb_v[...].astype(F32)], axis=0).astype(BF)
 
-    pl.semaphore_wait(barrier, len(peers))
-    for r in near:
-        b_copy(r).start()
-    for copy in (za_copy, m_copy):
-        for slot, dz in ((1, 1), (2, NZ - 1)):
-            copy(0, slot, at_z(z + dz)).start()
-
-    def forward_a(c):
-        for copy in (m_copy, za_copy):
-            copy(0, c, at_z(z)).wait_recv()
-        for copy in (m_copy, za_copy):
-            copy(c, c + 2, at_z(z + jnp.where(c % 2 == 1, 1, NZ - 1))).start()
-
-    def forward_b(c):
-        @pl.when(c == 0)
-        def _():
-            for r in near:
-                b_arrival(r).wait_recv()
-            zb_copy(0, 1, at_z(z + 1)).start()
-            zb_copy(0, 2, at_z(z + NZ - 1)).start()
-
-        @pl.when(c > 0)
-        def _():
-            zb_copy(0, c, at_z(z)).wait_recv()
-            zb_copy(c, c + 2, at_z(z + jnp.where(c % 2 == 1, 1, NZ - 1))).start()
-
-    def select_a(c):
-        @pl.when(c >= NZ - 2)
-        def _():
-            for copy in (m_copy, za_copy):
-                copy(0, c, at_z(z)).wait_recv()
-
+    def selection(c):
         info = meta[c].astype(F32)
         rel = info[0:8] - jnp.asarray(NX * NX * z, F32)
         comb = info[8:16]
@@ -269,6 +238,44 @@
         xsa[c] = dot(sel[c], ta[c]).astype(BF)
         xin[c, y, rows48(x)] = xsa[c, rows48(x)]
         wtr[c, x, :, 0:CAP] = wts[c, x, :, 0:CAP]
+
+    selection(0)
+    pl.semaphore_wait(barrier, len(peers))
+    for r in near:
+        b_copy(r).start()
+    for copy in (za_copy, m_copy):
+        for slot, dz in ((1, 1), (2, NZ - 1)):
+            copy(0, slot, at_z(z + dz)).start()
+
+    def forward_a(c):
+        for copy in (m_copy, za_copy):
+            copy(0, c, at_z(z)).wait_recv()
+        for copy in (m_copy, za_copy):
+            copy(c, c + 2, at_z(z + jnp.where(c % 2 == 1, 1, NZ - 1))).start()
+
+    def forward_b(c):
+        @pl.when(c == 0)
+        def _():
+            for r in near:
+                b_arrival(r).wait_recv()
+            zb_copy(0, 1, at_z(z + 1)).start()
+            zb_copy(0, 2, at_z(z + NZ - 1)).start()
+
+        @pl.when(c > 0)
+        def _():
+            zb_copy(0, c, at_z(z)).wait_recv()
+            zb_copy(c, c + 2, at_z(z + jnp.where(c % 2 == 1, 1, NZ - 1))).start()
+
+    def select_a(c):
+        @pl.when(c >= NZ - 2)
+        def _():
+            for copy in (m_copy, za_copy):
+                copy(0, c, at_z(z)).wait_recv()
+
+        @pl.when(c > 0)
+        def _():
+            selection(c)
+
         for r in near:
             to_x(xa_copy, c, r).start()
         for r in near:
@@ -314,18 +321,20 @@
             )
             hid[:, cols] = (gate / (1.0 + jnp.exp(-gate)) * up * scale).astype(BF)
         h = hid[...]
-        for j in range(NT):
+        for r in (2, 1, 3, 0):
+            j = (y + r) % NT
             for n in range(SLICE // 256):
                 lo = n * 256
-                part = dot(h, wd[:, j * SLICE + lo : j * SLICE + lo + 256]).astype(BF)
+                part = dot(h, wd[:, pl.ds(pl.multiple_of(j * SLICE + lo, 128), 256)]).astype(BF)
                 split = min(max(AR - lo, 0), 256)
                 if split:
                     pa[c, j, :, lo : lo + split] = part[:, :split]
                 if split < 256:
-                    at = BR * j + lo + split - AR
-                    pb[c, :, at : at + 256 - split] = part[:, split:]
-        for k in range(2):
-            s1_copy(c, k).start()
+                    at = pl.multiple_of(BR * j + lo + split - AR, 128)
+                    pb[c, :, pl.ds(at, 256 - split)] = part[:, split:]
+            if r == 1:
+                for k in range(2):
+                    s1_copy(c, k).start()
 
     def scatter1(c):
         for k in range(2):

time: 96.8 us -> 96 us (level)
  Pallas kernels: 95.1 us -> 93.7 us
    pallas_call x1, Pallas kernels: 95.1 us -> 93.7 us  [per_device(): pl.pallas_call(kernel, out_shape=jax.ShapeDtypeStruct((TOK, SLICE), BF),...]
where the time goes in v5:
time: 96 us; the launch traced here: 95.2 us
  Pallas kernels  93.7 us (98%)
  local copies, waits for them, and re-layouts  1.57 us (2%)
    pallas_call x1, Pallas kernels, per_device(): pl.pallas_call(kernel, out_shape=jax.ShapeDtypeStruct((TOK, SLICE), BF),...  93.7 us

profile of v5, /device:TPU:4, one launch (start us, length us, event | category | flops | bytes accessed | tf_op | source)
XLA Modules:
  0.0 95.2 jit_solution(9709431826222957991)
XLA Ops:
  0.0 93.7 %moe.1 = bf16[128,512]{1,0:T(8,128)(2,1)} custom-call(bf16[128,512]{1,0:T(8,128)(2,1)} %tok_hbm.1, s32[8,128]{1,0:T(8,128)} %bitcast.8, bf16[8,128]{1,0:T(8,128)(2,1)} %bitcast.9, bf16[768,2048]{1,0:T(8,128)(2,1)} %bitcast.5, bf16[768,2048]{1,0:T(8,128)(2,1)} %bitcast.6, bf16[768,2048]{1,0:T(8,128)(2,1)} %bitcast.7), custom_call_target="tpu_custom_call" | custom-call | tf_op jit(solution)/shard_map/moe/pallas_call | solution.py:469
  93.7 1.6 %copy.8 = bf16[128,512]{1,0:T(8,128)(2,1)} copy(bf16[128,512]{1,0:T(8,128)(2,1)} %moe.1) | data formatting | bytes 262144

commit v6 on v5

--- a/solution.py
+++ b/solution.py
@@ -332,7 +332,7 @@
                 if split < 256:
                     at = pl.multiple_of(BR * j + lo + split - AR, 128)
                     pb[c, :, pl.ds(at, 256 - split)] = part[:, split:]
-            if r == 1:
+            if r == 2:
                 for k in range(2):
                     s1_copy(c, k).start()
 

time: 96 us -> 96.4 us (level)
  Pallas kernels: 93.7 us -> 94.7 us
    pallas_call x1, Pallas kernels: 93.7 us -> 94.7 us  [per_device(): pl.pallas_call(kernel, out_shape=jax.ShapeDtypeStruct((TOK, SLICE), BF),...]
where the time goes in v6:
time: 96.4 us; the launch traced here: 96.3 us
  Pallas kernels  94.7 us (98%)
  local copies, waits for them, and re-layouts  1.57 us (2%)
    pallas_call x1, Pallas kernels, per_device(): pl.pallas_call(kernel, out_shape=jax.ShapeDtypeStruct((TOK, SLICE), BF),...  94.7 us

profile of v6, /device:TPU:4, one launch (start us, length us, event | category | flops | bytes accessed | tf_op | source)
XLA Modules:
  0.0 96.3 jit_solution(13248539668233878317)
XLA Ops:
  0.0 94.7 %moe.1 = bf16[128,512]{1,0:T(8,128)(2,1)} custom-call(bf16[128,512]{1,0:T(8,128)(2,1)} %tok_hbm.1, s32[8,128]{1,0:T(8,128)} %bitcast.8, bf16[8,128]{1,0:T(8,128)(2,1)} %bitcast.9, bf16[768,2048]{1,0:T(8,128)(2,1)} %bitcast.5, bf16[768,2048]{1,0:T(8,128)(2,1)} %bitcast.6, bf16[768,2048]{1,0:T(8,128)(2,1)} %bitcast.7), custom_call_target="tpu_custom_call" | custom-call | tf_op jit(solution)/shard_map/moe/pallas_call | solution.py:469
  94.7 1.6 %copy.8 = bf16[128,512]{1,0:T(8,128)(2,1)} copy(bf16[128,512]{1,0:T(8,128)(2,1)} %moe.1) | data formatting | bytes 262144
